TPU v7x, 32 devices: a 4x4x1 block of a 4x4x8 slice. The times are simulated.
32 devices in a mesh: dp: 1 (over z), yax: 4 (over y), xax: 8 (over x, core).
Axes of the slice: x: 4, y: 4, z: 1, core: 2. Of those that a mesh axis runs over, the one named last changes fastest.
The devices are a block of a 4x4x8 slice.
Arguments:
- hidden: bfloat16 [1024, 1024], P('dp', 'xax')
- cache_len: int32 [1024], P('dp')
- k_cache: bfloat16 [1024, 4096, 64], P(('dp', 'yax', 'xax'))
- v_cache: bfloat16 [1024, 4096, 64], P(('dp', 'yax', 'xax'))
- g_attn: float32 [1024], P('xax')
- w_query: bfloat16 [1024, 1024], P('xax', 'yax')
- w_key: bfloat16 [1024, 64], P('xax')
- w_value: bfloat16 [1024, 64], P('xax')
- w_gate: bfloat16 [1024, 4096], P('xax', 'yax')
- w_up: bfloat16 [1024, 4096], P('xax', 'yax')
- w_out: bfloat16 [1024, 1024], P('yax', 'xax')
- w_down: bfloat16 [4096, 1024], P('yax', 'xax')
- g_final: float32 [1024], P('xax')
- embedding: bfloat16 [50304, 1024], P('yax', 'xax')
Outputs:
- output 1: bfloat16 [1024, 64], P(('dp', 'yax', 'xax'))
- output 2: bfloat16 [1024, 64], P(('dp', 'yax', 'xax'))
- output 3: float32 [1024, 50304], P('dp', ('yax', 'xax'))
- output 4: float32 [1024], P('dp')
All inputs are finite; a program needn't handle non-finite values.
Results may differ from a plain program's by a relative error of at most 0.00831753.
Values are sent between devices in bfloat16 or wider.
A program may use at most 768 MiB of HBM per device.

v0:
```python
import jax
import jax.numpy as jnp
from jax import lax
from jax.sharding import PartitionSpec as P

EPS = 1e-6
ROPE_BASE = 10000.0


def rope_angle(positions, head_dim):
    half_dim = head_dim // 2
    inv_freq = ROPE_BASE ** (-(jnp.arange(half_dim, dtype=jnp.float32) * 2.0) / head_dim)
    return positions.astype(jnp.float32)[:, None] * inv_freq[None, :]


def rotary(values_in, angles):
    half_dim = values_in.shape[-1] // 2
    cos_a = jnp.cos(angles)
    sin_a = jnp.sin(angles)
    first = values_in[..., :half_dim]
    second = values_in[..., half_dim:]
    return jnp.concatenate([first * cos_a - second * sin_a, second * cos_a + first * sin_a], axis=-1)


def sharded_norm(values_in, gain, width):
    stats = jnp.stack([jnp.sum(values_in, axis=-1), jnp.sum(values_in * values_in, axis=-1)])
    stats = lax.psum(stats, "xax")
    row_mean = stats[0] / width
    row_var = stats[1] / width - row_mean * row_mean
    return (values_in - row_mean[:, None]) * lax.rsqrt(row_var + EPS)[:, None] * gain


def attend_local(query, k_cache, v_cache, key_new, value_new, lengths):
    score_scale = query.shape[-1] ** -0.5
    scores = jnp.einsum("bhe,bse->bhs", query, k_cache, preferred_element_type=jnp.float32) * score_scale
    score_new = jnp.einsum("bhe,be->bh", query, key_new, preferred_element_type=jnp.float32) * score_scale
    valid = jnp.arange(k_cache.shape[1])[None, None, :] < lengths[:, None, None]
    row_max = jnp.maximum(jnp.max(jnp.where(valid, scores, -jnp.inf), axis=-1), score_new)
    weights = jnp.where(valid, jnp.exp(scores - row_max[..., None]), 0.0)
    weight_new = jnp.exp(score_new - row_max)
    denominator = jnp.sum(weights, axis=-1) + weight_new
    prob_all = (weights / denominator[..., None]).astype(jnp.bfloat16)
    prob_new = (weight_new / denominator).astype(jnp.bfloat16)
    attn_out = jnp.einsum("bhs,bse->bhe", prob_all, v_cache, preferred_element_type=jnp.float32)
    attn_out = attn_out + prob_new.astype(jnp.float32)[..., None] * value_new.astype(jnp.float32)[:, None, :]
    return attn_out.astype(jnp.bfloat16)


def solution(mesh):
    y_size = mesh.shape["yax"]
    x_size = mesh.shape["xax"]
    row_spec = P(("dp", "yax", "xax"))

    def local_step(hidden, cache_len, k_cache, v_cache, g_attn, w_query, w_key, w_value,
                   w_gate, w_up, w_out, w_down, g_final, embedding):
        rows = hidden.shape[0]
        width = hidden.shape[1] * x_size
        own_rows = k_cache.shape[0]
        head_dim = k_cache.shape[2]
        q_cols = w_query.shape[1]
        kv_end = q_cols + 2 * head_dim
        ff_end = kv_end + w_gate.shape[1]
        y_idx = lax.axis_index("yax")
        x_idx = lax.axis_index("xax")
        own_start = (y_idx * x_size + x_idx) * own_rows

        residual = hidden.astype(jnp.float32)
        normed = sharded_norm(residual, g_attn, width).astype(jnp.bfloat16)
        proj_part = jnp.concatenate([
            jnp.dot(normed, w_query, preferred_element_type=jnp.float32),
            jnp.dot(normed, w_key, preferred_element_type=jnp.float32),
            jnp.dot(normed, w_value, preferred_element_type=jnp.float32),
            jnp.dot(normed, w_gate, preferred_element_type=jnp.float32),
            jnp.dot(normed, w_up, preferred_element_type=jnp.float32)], axis=1)
        projected = lax.psum(proj_part, "xax").astype(jnp.bfloat16)
        angles = rope_angle(cache_len, head_dim)
        query = projected[:, :q_cols].astype(jnp.float32).reshape(rows, q_cols // head_dim, head_dim)
        query = rotary(query, angles[:, None, :]).astype(jnp.bfloat16)
        key_new = rotary(projected[:, q_cols:q_cols + head_dim].astype(jnp.float32), angles).astype(jnp.bfloat16)
        value_new = projected[:, q_cols + head_dim:kv_end]
        gate = projected[:, kv_end:ff_end]
        up_val = projected[:, ff_end:]

        query_grp = lax.all_to_all(query, "yax", 0, 1, tiled=True)
        query_own = lax.dynamic_slice_in_dim(query_grp, x_idx * own_rows, own_rows, axis=0)
        key_own = lax.dynamic_slice_in_dim(key_new, own_start, own_rows, axis=0)
        value_own = lax.dynamic_slice_in_dim(value_new, own_start, own_rows, axis=0)
        len_own = lax.dynamic_slice_in_dim(cache_len, own_start, own_rows, axis=0)
        attn_own = attend_local(query_own, k_cache, v_cache, key_own, value_own, len_own)
        attn_grp = lax.all_gather(attn_own, "xax", axis=0, tiled=True)
        attn_heads = lax.all_to_all(attn_grp, "yax", 1, 0, tiled=True).reshape(rows, q_cols)

        mlp_act = (jax.nn.silu(gate.astype(jnp.float32)) * up_val.astype(jnp.float32)).astype(jnp.bfloat16)
        branch_sum = (jnp.dot(attn_heads, w_out, preferred_element_type=jnp.float32)
                      + jnp.dot(mlp_act, w_down, preferred_element_type=jnp.float32))
        residual_out = residual + lax.psum(branch_sum, "yax")
        final_norm = sharded_norm(residual_out, g_final, width).astype(jnp.bfloat16)
        logit_part = jnp.einsum("bd,vd->bv", final_norm, embedding, preferred_element_type=jnp.float32)
        logits = lax.psum_scatter(logit_part, "xax", scatter_dimension=1, tiled=True)
        row_max = lax.pmax(jnp.max(logits, axis=1), ("yax", "xax"))
        sum_exp = lax.psum(jnp.sum(jnp.exp(logits - row_max[:, None]), axis=1), ("yax", "xax"))
        log_norm = row_max + jnp.log(sum_exp)
        return key_own, value_own, logits - log_norm[:, None], log_norm

    in_specs = (P("dp", "xax"), P("dp"), row_spec, row_spec, P("xax"), P("xax", "yax"),
                P("xax", None), P("xax", None), P("xax", "yax"), P("xax", "yax"),
                P("yax", "xax"), P("yax", "xax"), P("xax"), P("yax", "xax"))
    out_specs = (row_spec, row_spec, P("dp", ("yax", "xax")), P("dp"))
    return jax.shard_map(local_step, mesh=mesh, in_specs=in_specs, out_specs=out_specs, check_vma=False)
```

profile of v0, /device:TPU:97, one launch (start us, length us, event | category | flops | bytes accessed | tf_op | source)
XLA Modules:
  0.0 768.6 jit_solution(1074630308356095306)
XLA Ops:
  7.2 0.0 copy-start
  7.2 0.0 copy-start.2
  7.2 0.0 copy-start.8
  7.2 1.4 convert_reduce_fusion
  8.6 14.1 %psum.35 = f32[2,1024]{1,0:T(2,128)S(1)} all-reduce(f32[2,1024]{1,0:T(2,128)S(1)} %pad_maximum_fusion.1), channel_id=1, replica_groups=mesh['dp'=1,'yax'=4,'xax'=8] {'xax'}, use_global_device_ids=true, to_apply=%region_2.0 | all-reduce | flops 2048 | bytes 16384 | tf_op jit(solution)/shard_map/psum | solution.py:27
  22.7 0.0 copy-start.4
  22.8 2.4 fusion.43
  25.2 2.2 fusion.41
  27.4 2.2 fusion.39
  29.7 3.8 fusion.37
  33.5 0.0 copy-done.8
  33.5 2.8 fusion.35
  36.3 11.0 %concatenate.11 = f32[1024,2432]{1,0:T(8,128)} concatenate(f32[1024,256]{1,0:T(8,128)} %fusion.43, f32[1024,64]{1,0:T(8,128)} %fusion.41, f32[1024,64]{1,0:T(8,128)} %fusion.39, f32[1024,1024]{1,0:T(8,128)} %fusion.37, f32[1024,1024]{1,0:T(8,128)} %fusion.35), dimensions={1} | concatenate | bytes 19922944 | tf_op jit(solution)/shard_map/concatenate | solution.py:69
  47.3 107.5 %all-reduce.6 = bf16[1024,2432]{1,0:T(8,128)(2,1)} all-reduce(f32[1024,2432]{1,0:T(8,128)} %concatenate.11), channel_id=1, replica_groups=mesh['dp'=1,'yax'=4,'xax'=8] {'xax'}, use_global_device_ids=true, to_apply=%region_3.0 | all-reduce | flops 2490368 | bytes 14942208 | tf_op jit(solution)/shard_map/psum | solution.py:75
  154.8 2.1 fusion.46
  156.9 2.2 slice_convert_fusion
  159.0 2.6 copy.50
  161.6 4.7 multiply_cosine_fusion
  166.3 1.9 copy.52
  168.1 1.9 copy.51
  170.0 1.4 subtract_convert_fusion
  171.4 0.9 pad_maximum_fusion
  172.3 2.3 copy.53
  174.6 2.6 reshape.151
  177.2 5.6 all-to-all-start
  182.8 0.1 dynamic_slice.14
  182.9 0.8 iota_compare_fusion
  183.7 1.3 fusion.45
  185.0 5.7 all-to-all-done
  190.7 2.5 reshape.152
  193.2 1.6 copy.54
  194.8 0.2 fusion.22
  195.0 7.3 select_reduce_fusion
  202.3 3.2 copy-done.1
  205.5 0.0 copy-done.3
  205.5 2.5 fusion.1
  208.0 10.7 %fusion.12 = bf16[32,16,64]{2,1,0:T(8,128)(2,1)S(1)} fusion(bf16[32,4096,64]{1,2,0:T(8,128)(2,1)} %param.17, f32[32,16,4096]{2,1,0:T(8,128)} %copy-done.1, f32[32,16]{1,0:T(8,128)S(1)} %get-tuple-element.29, f32[32,16]{1,0:T(8,128)S(1)} %multiply_maximum_fusion, pred[32,4096]{1,0:T(8,128)(4,1)S(1)} %copy-done.3, f32[32,64]{1,0:T(8,128)S(1)} %get-tuple-element.20, ...), kind=kOutput, calls=%fused_computation.19 | convolution fusion | flops 279019520 | bytes 25376768 | tf_op jit(solution)/shard_map/bhs,bse->bhe/dot_general | solution.py:44
  218.7 20.4 %all_gather.3 = bf16[256,16,64]{2,1,0:T(8,128)(2,1)} all-gather(bf16[32,16,64]{2,1,0:T(8,128)(2,1)S(1)} %fusion.12), channel_id=1, replica_groups=mesh['dp'=1,'yax'=4,'xax'=8] {'xax'}, dimensions={0}, use_global_device_ids=true | all-gather | bytes 589824 | tf_op jit(solution)/shard_map/all_gather | solution.py:90
  239.1 2.8 copy.55
  241.9 4.2 all-to-all-start.1
  246.1 0.0 copy-start.5
  246.1 0.0 copy-start.6
  246.1 0.1 all-reduce.5.cloned.1.call-start
  246.2 4.5 fusion.9
  250.6 2.1 all-to-all-done.1
  252.7 1.4 copy.56
  254.2 0.1 copy.64
  254.3 2.2 convolution_add_fusion
  256.4 0.1 all-reduce.5.cloned.1.call-update
  256.5 40.3 %all-reduce.5.cloned.1.call-done = f32[1024,128]{1,0:T(8,128)} async-done(((f32[1024,128]{1,0:T(8,128)}), f32[1024,128]{1,0:T(8,128)}) %all-reduce.5.cloned.1.call-update) | async-done | bytes 524304 | tf_op jit(solution)/shard_map/psum | solution.py:96
  296.8 1.4 fusion.21
  298.2 15.1 %psum.38 = f32[2,1024]{1,0:T(2,128)S(1)} all-reduce(f32[2,1024]{1,0:T(2,128)S(1)} %pad_maximum_fusion.2), channel_id=1, replica_groups=mesh['dp'=1,'yax'=4,'xax'=8] {'xax'}, use_global_device_ids=true, to_apply=%region_9.10 | all-reduce | flops 2048 | bytes 16384 | tf_op jit(solution)/shard_map/psum | solution.py:27
  313.3 21.0 %fusion.17 = f32[1024,12576]{0,1:T(8,128)} fusion(bf16[12576,128]{1,0:T(8,128)(2,1)S(1)} %copy-done, f32[128]{0:T(128)S(1)} %copy-done.6, f32[1024]{0:T(1024)S(1)} %add_rsqrt_fusion, f32[1024]{0:T(1024)S(1)} %bitcast.42, f32[1024,128]{1,0:T(8,128)} %all-reduce.5.cloned.1.call-done, bf16[1024,128]{1,0:T(8,128)(2,1)S(1)} %copy-done.2), kind=kOutput, calls=%fused_computation.39 | convolution fusion | flops 3297509376 | bytes 55525888 | tf_op jit(solution)/shard_map/bd,vd->bv/dot_general | solution.py:98
  334.3 294.7 %fusion = f32[1024,1584]{0,1:T(8,128)} fusion(f32[1024,12576]{0,1:T(8,128)} %fusion.17), kind=kCustom, calls=%all-reduce-scatter | all-reduce-scatter fusion | flops 12976129 | bytes 57999872
  629.0 1.8 slice.65
  630.8 4.4 collective-permute-start
  635.2 0.6 dynamic-slice.4
  636.5 3.1 collective-permute-done
  639.5 19.0 %concatenate.14 = f32[1024,1668]{0,1:T(8,128)} concatenate(f32[1024,84]{0,1:T(8,128)} %collective-permute-done, f32[1024,1584]{0,1:T(8,128)} %fusion), dimensions={1} | concatenate | bytes 13664256
  658.6 3.6 dynamic-slice_reduce_fusion
  662.1 44.6 %pmax.7 = f32[1024]{0:T(1024)S(1)} all-reduce(f32[1024]{0:T(1024)S(1)} %dynamic-slice_reduce_fusion), channel_id=1, replica_groups=mesh['dp'=1,'yax'=4,'xax'=8] {'yax','xax'}, use_global_device_ids=true, to_apply=%region_12.13 | all-reduce | flops 1024 | bytes 8192 | tf_op jit(solution)/shard_map/pmax | solution.py:100
  706.7 4.1 exponential_reduce_fusion
  710.8 43.7 %psum.39 = f32[1024]{0:T(1024)S(1)} all-reduce(f32[1024]{0:T(1024)S(1)} %exponential_reduce_fusion), channel_id=1, replica_groups=mesh['dp'=1,'yax'=4,'xax'=8] {'yax','xax'}, use_global_device_ids=true, to_apply=%region_14.15 | all-reduce | flops 1024 | bytes 8192 | tf_op jit(solution)/shard_map/psum | solution.py:101
  754.5 7.1 dynamic-slice_subtract_fusion
  (26 shorter events, 0.1 us)
Async XLA Ops:
  7.2 306.1 %copy-start = (bf16[12576,128]{1,0:T(8,128)(2,1)S(1)}, bf16[12576,128]{1,0:T(8,128)(2,1)}, u32[]{:S(2)}) copy-start(bf16[12576,128]{1,0:T(8,128)(2,1)} %param.27) | copy-start | bytes 9658372
  7.2 26.3 %copy-start.2 = (bf16[1024,128]{1,0:T(8,128)(2,1)S(1)}, bf16[1024,128]{1,0:T(8,128)(2,1)}, u32[]{:S(2)}) copy-start(bf16[1024,128]{1,0:T(8,128)(2,1)} %param.14) | copy-start | bytes 786436
  7.2 26.3 %copy-start.8 = (f32[128]{0:T(128)S(1)}, f32[128]{0:T(128)}, u32[]{:S(2)}) copy-start(f32[128]{0:T(128)} %param.18) | copy-start | bytes 1540
  22.7 10.8 %copy-start.4 = (bf16[128,1024]{1,0:T(8,128)(2,1)S(1)}, bf16[128,1024]{1,0:T(8,128)(2,1)}, u32[]{:S(2)}) copy-start(bf16[128,1024]{1,0:T(8,128)(2,1)} %param.23) | copy-start | bytes 786436
  47.3 111.8 %copy-start.10 = (s32[1024]{0:T(1024)S(1)}, s32[1024]{0:T(1024)}, u32[]{:S(2)}) copy-start(s32[1024]{0:T(1024)} %param.15) | copy-start | bytes 12292
  177.2 13.5 %all-to-all-start = ((bf16[4,2,32768]{2,1,0:T(2,128)(2,1)}), bf16[4,2,32768]{2,1,0:T(2,128)(2,1)}, u32[]{:S(2)}, u32[]{:S(2)}) async-start(bf16[4,2,32768]{2,1,0:T(2,128)(2,1)} %reshape.151), calls=%async_computation | async-start | bytes 1048576 | tf_op jit(solution)/shard_map/all_to_all | solution.py:84
  185.0 17.2 %copy-start.9 = (bf16[32,64]{1,0:T(8,128)(2,1)}, bf16[32,64]{1,0:T(8,128)(2,1)S(1)}, u32[]{:S(2)}) copy-start(bf16[32,64]{1,0:T(8,128)(2,1)S(1)} %get-tuple-element.40) | copy-start | bytes 12292
  195.0 10.5 %copy-start.3 = (pred[32,4096]{1,0:T(8,128)(4,1)S(1)}, pred[32,4096]{1,0:T(8,128)(4,1)}, u32[]{:S(2)}) copy-start(pred[32,4096]{1,0:T(8,128)(4,1)} %iota_compare_fusion) | copy-start | bytes 393220
  202.2 3.2 copy-start.1
  241.9 10.8 %all-to-all-start.1 = ((bf16[256,16,64]{0,2,1:T(8,128)(2,1)}), bf16[256,16,64]{0,2,1:T(8,128)(2,1)}, u32[]{:S(2)}, u32[]{:S(2)}) async-start(bf16[256,16,64]{0,2,1:T(8,128)(2,1)} %copy.55), calls=%async_computation.1 | async-start | bytes 1048576 | tf_op jit(solution)/shard_map/all_to_all | solution.py:91
  246.1 8.2 %copy-start.5 = (bf16[256,128]{1,0:T(8,128)(2,1)S(1)}, bf16[256,128]{1,0:T(8,128)(2,1)}, u32[]{:S(2)}) copy-start(bf16[256,128]{1,0:T(8,128)(2,1)} %param.24) | copy-start | bytes 196612
  246.1 67.2 %copy-start.6 = (f32[128]{0:T(128)S(1)}, f32[128]{0:T(128)}, u32[]{:S(2)}) copy-start(f32[128]{0:T(128)} %param.26) | copy-start | bytes 1540
  246.1 50.7 %all-reduce.5.cloned.1.call-start = ((), (), s32[]{:S(2)}) async-start(), calls=%async_computation.2 | async-start | bytes 1048576 | tf_op jit(solution)/shard_map/psum | solution.py:96
  334.3 300.9 %copy-start.11 = (u32[32]{0:T(128)S(1)}, u32[32]{0:T(128)}, u32[]{:S(2)}) copy-start(u32[32]{0:T(128)} %constant.45) | copy-start | bytes 388
  630.8 8.8 %collective-permute-start = (f32[1024,84]{0,1:T(8,128)}, f32[1024,84]{0,1:T(8,128)}, u32[]{:S(2)}, u32[]{:S(2)}) collective-permute-start(f32[1024,84]{0,1:T(8,128)} %slice.65), channel_id=1, source_target_pairs={{0,1},{1,2},{2,3},{3,4},{4,5},{5,6},{6,7},{8,9},{9,10},{10,11},{11... | collective-permute-start | bytes 1032200
  754.5 7.1 copy-start.7
Sparse Core Ops, SparseCore 0:
  256.6 40.0 all-reduce.4
where the time goes:
time: 771 us; the launch traced here: 769 us
  blocking collectives  540 us (70%)
  matrix products  59.3 us (8%)
  local copies, waits for them, and re-layouts  55.3 us (7%)
  waiting for transfers between devices  51.1 us (7%)
  other arithmetic  33.4 us (4%)
  between operations  15 us (2%)
  starting transfers between devices  14.3 us (2%)
    unnamed x1, blocking collectives  295 us
    psum x1, blocking collectives, local_step(): projected = lax.psum(proj_part, 'xax').astype(jnp.bfloat16)  108 us
    pmax x1, blocking collectives, local_step(): row_max = lax.pmax(jnp.max(logits, axis=1), ('yax', 'xax'))  44.6 us
    psum x1, blocking collectives, local_step(): lax.psum(jnp.sum(jnp.exp(logits - row_max[:, None]), axis=1), ('yax', 'xa...  43.7 us
    psum x1, waiting for transfers between devices, local_step(): residual_out = residual + lax.psum(branch_sum, 'yax')  40.3 us
    unnamed x30, local copies, waits for them, and re-layouts  29.8 us
    psum x2, blocking collectives, sharded_norm(): stats = lax.psum(stats, 'xax')  29.1 us
    dot_general x1, matrix products, local_step(): jnp.einsum('bd,vd->bv', final_norm, embedding, preferred_element_type=jnp...  21 us
  transfers between devices with their start and end apart: 4, of which 4 were waited for; matrix products, arithmetic and copies ran while one was open for 1% of the time, Pallas kernels for 0%

commit v1 on v0

--- a/solution.py
+++ b/solution.py
@@ -64,6 +64,7 @@
         x_idx = lax.axis_index("xax")
         own_start = (y_idx * x_size + x_idx) * own_rows
 
+        embed_full = lax.all_to_all(embedding, "xax", 0, 1, tiled=True)
         residual = hidden.astype(jnp.float32)
         normed = sharded_norm(residual, g_attn, width).astype(jnp.bfloat16)
         proj_part = jnp.concatenate([
@@ -95,10 +96,13 @@
                       + jnp.dot(mlp_act, w_down, preferred_element_type=jnp.float32))
         residual_out = residual + lax.psum(branch_sum, "yax")
         final_norm = sharded_norm(residual_out, g_final, width).astype(jnp.bfloat16)
-        logit_part = jnp.einsum("bd,vd->bv", final_norm, embedding, preferred_element_type=jnp.float32)
-        logits = lax.psum_scatter(logit_part, "xax", scatter_dimension=1, tiled=True)
-        row_max = lax.pmax(jnp.max(logits, axis=1), ("yax", "xax"))
-        sum_exp = lax.psum(jnp.sum(jnp.exp(logits - row_max[:, None]), axis=1), ("yax", "xax"))
+        final_full = lax.all_gather(final_norm, "xax", axis=1, tiled=True)
+        logits = jnp.einsum("bd,vd->bv", final_full, embed_full, preferred_element_type=jnp.float32)
+        part_max = jnp.max(logits, axis=1)
+        part_sum = jnp.sum(jnp.exp(logits - part_max[:, None]), axis=1)
+        parts = lax.all_gather(jnp.stack([part_max, part_sum]), ("yax", "xax"), axis=0)
+        row_max = jnp.max(parts[:, 0], axis=0)
+        sum_exp = jnp.sum(parts[:, 1] * jnp.exp(parts[:, 0] - row_max), axis=0)
         log_norm = row_max + jnp.log(sum_exp)
         return key_own, value_own, logits - log_norm[:, None], log_norm
 

time: 771 us -> 399 us (0.52)
  blocking collectives: 540 us -> 234 us
  local copies, waits for them, and re-layouts: 55.3 us -> 29.8 us
  matrix products: 59.3 us -> 37.1 us
  other arithmetic: 33.4 us -> 19.1 us
    unnamed x1 -> x0, blocking collectives: 295 us -> none
    all_to_all x0 -> x1, blocking collectives: none -> 49.5 us  [local_step(): embed_full = lax.all_to_all(embedding, 'xax', 0, 1, tiled=True)]
    pmax x1 -> x0, blocking collectives: 44.6 us -> none  [local_step(): row_max = lax.pmax(jnp.max(logits, axis=1), ('yax', 'xax'))]
    psum x1 -> x0, blocking collectives: 43.7 us -> none  [local_step(): lax.psum(jnp.sum(jnp.exp(logits - row_max[:, None]), axis=1), ('yax', 'xa...]
    all_gather x0 -> x1, blocking collectives: none -> 28.1 us  [local_step(): lax.all_gather(jnp.stack([part_max, part_sum]), ('yax', 'xax'), axis=0)]
    unnamed x30 -> x33, local copies, waits for them, and re-layouts: 29.8 us -> 6.76 us
    dot_general x1, matrix products: 21 us -> 5.26 us  [local_step(): jnp.einsum('bd,vd->bv', final_full, embed_full, preferred_element_type=jn...]
    all_to_all x0 -> x2, local copies, waits for them, and re-layouts: none -> 8.72 us  [local_step(): embed_full = lax.all_to_all(embedding, 'xax', 0, 1, tiled=True)]
  transfers between devices with their start and end apart: 4 -> 4, of which waited for: 4 -> 3; matrix products, arithmetic and copies ran while one was open for 1% -> 3% of each run, Pallas kernels for 0% -> 0%
where the time goes in v1:
time: 399 us; the launch traced here: 394 us
  blocking collectives  234 us (59%)
  waiting for transfers between devices  49.5 us (12%)
  matrix products  37.1 us (9%)
  local copies, waits for them, and re-layouts  29.8 us (7%)
  other arithmetic  19.1 us (5%)
  between operations  14.5 us (4%)
  starting transfers between devices  9.34 us (2%)
    psum x1, blocking collectives, local_step(): projected = lax.psum(proj_part, 'xax').astype(jnp.bfloat16)  108 us
    all_to_all x1, blocking collectives, local_step(): embed_full = lax.all_to_all(embedding, 'xax', 0, 1, tiled=True)  49.5 us
    psum x1, waiting for transfers between devices, local_step(): residual_out = residual + lax.psum(branch_sum, 'yax')  40.2 us
    psum x2, blocking collectives, sharded_norm(): stats = lax.psum(stats, 'xax')  28.9 us
    all_gather x1, blocking collectives, local_step(): lax.all_gather(jnp.stack([part_max, part_sum]), ('yax', 'xax'), axis=0)  28.1 us
    all_gather x1, blocking collectives, local_step(): attn_grp = lax.all_gather(attn_own, 'xax', axis=0, tiled=True)  20.4 us
    dot_general x1, matrix products, attend_local(): jnp.einsum('bhs,bse->bhe', prob_all, v_cache, preferred_element_type=jnp....  10.7 us
    concatenate x1, local copies, waits for them, and re-layouts, local_step(): jnp.concatenate([jnp.dot(normed, w_query, preferred_element_type=jnp.floa...  10.4 us
  transfers between devices with their start and end apart: 4, of which 3 were waited for; matrix products, arithmetic and copies ran while one was open for 3% of the time, Pallas kernels for 0%

profile of v1, /device:TPU:97, one launch (start us, length us, event | category | flops | bytes accessed | tf_op | source)
XLA Modules:
  0.0 393.8 jit_solution(4747565977150623816)
XLA Ops:
  7.2 0.0 copy-start
  7.2 0.0 copy-start.3
  7.2 0.0 copy-start.9
  7.3 1.3 convert_reduce_fusion
  8.6 14.1 %psum.28 = f32[2,1024]{1,0:T(2,128)S(1)} all-reduce(f32[2,1024]{1,0:T(2,128)S(1)} %pad_maximum_fusion.1), channel_id=1, replica_groups=mesh['dp'=1,'yax'=4,'xax'=8] {'xax'}, use_global_device_ids=true, to_apply=%region_2.0 | all-reduce | flops 2048 | bytes 16384 | tf_op jit(solution)/shard_map/psum | solution.py:27
  22.7 3.8 fusion.33
  26.5 3.8 fusion.35
  30.3 0.5 fusion.41
  30.8 0.5 fusion.37
  31.2 0.5 fusion.39
  31.7 10.4 %concatenate.11 = f32[1024,2432]{1,0:T(8,128)} concatenate(f32[1024,256]{1,0:T(8,128)S(1)} %fusion.41, f32[1024,64]{1,0:T(8,128)S(1)} %fusion.39, f32[1024,64]{1,0:T(8,128)S(1)} %fusion.37, f32[1024,1024]{1,0:T(8,128)} %fusion.35, f32[1024,1024]{1,0:T(8,128)} %fusion.33), dimensions={1} | concatenate | bytes 19922944 | tf_op jit(solution)/shard_map/concatenate | solution.py:70
  42.1 107.5 %all-reduce.4 = bf16[1024,2432]{1,0:T(8,128)(2,1)} all-reduce(f32[1024,2432]{1,0:T(8,128)} %concatenate.11), channel_id=1, replica_groups=mesh['dp'=1,'yax'=4,'xax'=8] {'xax'}, use_global_device_ids=true, to_apply=%region_3.0 | all-reduce | flops 2490368 | bytes 14942208 | tf_op jit(solution)/shard_map/psum | solution.py:76
  149.7 1.9 fusion.44
  151.6 1.1 slice_convert_fusion
  152.8 2.3 multiply_cosine_fusion
  155.1 0.2 copy.58
  155.3 0.2 copy.59
  155.4 0.3 copy.57
  155.8 0.1 subtract_convert_fusion
  156.0 0.7 copy.60
  156.7 1.5 reshape.163
  158.2 5.7 %all-to-all-start = ((bf16[4,2,32768]{2,1,0:T(2,128)(2,1)}), bf16[4,2,32768]{2,1,0:T(2,128)(2,1)S(1)}, u32[]{:S(2)}, u32[]{:S(2)}) async-start(bf16[4,2,32768]{2,1,0:T(2,128)(2,1)} %reshape.163), calls=%async_computation | async-start | bytes 1048576 | tf_op jit(solution)/shard_map/all_to_all | solution.py:85
  163.9 0.1 dynamic_slice.14
  164.0 0.1 iota_compare_fusion
  164.1 1.3 fusion.43
  165.4 6.3 %all-to-all-done = bf16[4,2,32768]{2,1,0:T(2,128)(2,1)S(1)} async-done(((bf16[4,2,32768]{2,1,0:T(2,128)(2,1)}), bf16[4,2,32768]{2,1,0:T(2,128)(2,1)S(1)}, u32[]{:S(2)}, u32[]{:S(2)}) %all-to-all-start) | async-done | bytes 524320 | tf_op jit(solution)/shard_map/all_to_all | solution.py:85
  171.8 0.7 reshape.164
  172.5 0.4 copy.61
  172.8 0.2 fusion.20
  173.0 7.2 %select_reduce_fusion = (f32[32,16]{1,0:T(8,128)S(1)}, f32[32,16,4096]{2,1,0:T(8,128)S(1)}) fusion(pred[32,4096]{1,0:T(8,128)(4,1)S(1)} %iota_compare_fusion, bf16[32,4096,64]{1,2,0:T(8,128)(2,1)} %param.16, bf16[256,16,64]{2,1,0:T(8,128)(2,1)S(1)} %bitcast.64, s32[]{:T(128)S(6)} %select_n.16), kind=kOutput, calls=%fused_computation.2 | convolution fusion | flops 274726400 | bytes 25430020 | tf_op jit(solution)/shard_map/bhe,bse->bhs/dot_general | solution.py:35
  180.3 3.2 copy-done.2
  183.5 2.5 fusion
  186.0 10.7 %fusion.11 = bf16[32,16,64]{2,1,0:T(8,128)(2,1)S(1)} fusion(bf16[32,4096,64]{1,2,0:T(8,128)(2,1)} %param.17, f32[32,16,4096]{2,1,0:T(8,128)} %copy-done.2, f32[32,16]{1,0:T(8,128)S(1)} %get-tuple-element.32, f32[32,16]{1,0:T(8,128)S(1)} %multiply_maximum_fusion, pred[32,4096]{1,0:T(8,128)(4,1)S(1)} %iota_compare_fusion, ...), kind=kOutput, calls=%fused_computation.18 | convolution fusion | flops 279019520 | bytes 25376768 | tf_op jit(solution)/shard_map/bhs,bse->bhe/dot_general | solution.py:44
  196.7 20.4 %all_gather.12 = bf16[256,16,64]{2,1,0:T(8,128)(2,1)S(1)} all-gather(bf16[32,16,64]{2,1,0:T(8,128)(2,1)S(1)} %fusion.11), channel_id=1, replica_groups=mesh['dp'=1,'yax'=4,'xax'=8] {'xax'}, dimensions={0}, use_global_device_ids=true | all-gather | bytes 589824 | tf_op jit(solution)/shard_map/all_gather | solution.py:91
  217.1 1.6 copy.62
  218.7 3.6 all-to-all-start.1
  222.3 0.0 copy-start.5
  222.3 0.0 copy-start.12
  222.3 0.1 all-reduce.3.cloned.1.call-start
  222.4 3.6 fusion.8
  226.0 2.9 all-to-all-done.1
  228.9 0.4 copy.63
  229.3 0.1 copy.75
  229.5 1.2 convolution_add_fusion
  230.6 0.1 all-reduce.3.cloned.1.call-update
  230.7 0.1 all-gather.4.cloned.1.call-start
  230.8 40.2 %all-reduce.3.cloned.1.call-done = f32[1024,128]{1,0:T(8,128)} async-done(((f32[1024,128]{1,0:T(8,128)}), f32[1024,128]{1,0:T(8,128)}) %all-reduce.3.cloned.1.call-update) | async-done | bytes 524304 | tf_op jit(solution)/shard_map/psum | solution.py:97
  270.9 1.4 fusion.16
  272.4 14.8 %psum.31 = f32[2,1024]{1,0:T(2,128)S(1)} all-reduce(f32[2,1024]{1,0:T(2,128)S(1)} %pad_maximum_fusion.2), channel_id=1, replica_groups=mesh['dp'=1,'yax'=4,'xax'=8] {'xax'}, use_global_device_ids=true, to_apply=%region_9.10 | all-reduce | flops 2048 | bytes 16384 | tf_op jit(solution)/shard_map/psum | solution.py:27
  287.2 2.1 multiply_convert_fusion
  289.3 0.1 all-gather.4.cloned.1.call-update
  289.4 2.9 all_to_all.45
  292.3 49.5 %all_to_all.52 = bf16[8,1572,128]{2,1,0:T(8,128)(2,1)S(1)} all-to-all(bf16[8,1572,128]{2,1,0:T(8,128)(2,1)S(1)} %all_to_all.45), channel_id=1, replica_groups=mesh['dp'=1,'yax'=4,'xax'=8] {'xax'}, dimensions={0} | all-to-all | bytes 6438912 | tf_op jit(solution)/shard_map/all_to_all | solution.py:67
  341.8 5.8 %copy.64 = bf16[1572,8,128]{2,1,0:T(8,128)(2,1)S(1)} copy(bf16[1572,8,128]{2,0,1:T(8,128)(2,1)S(1)} %bitcast.56) | data formatting | bytes 6438912 | tf_op jit(solution)/shard_map/all_to_all | solution.py:67
  347.6 0.3 pad.10
  347.9 0.8 copy.76
  348.7 0.0 all-gather.4.cloned.1.call-done
  348.8 5.3 %fusion.46 = (f32[1024]{0:T(1024)S(1)}, f32[1024,1572]{0,1:T(8,128)S(1)}) fusion(bf16[1024,1024]{1,0:T(8,128)(2,1)} %all-gather.4.cloned.1.call-done, bf16[1572,1024]{1,0:T(8,128)(2,1)S(1)} %bitcast.59), kind=kOutput, calls=%fused_computation.84 | convolution fusion | flops 3298331648 | bytes 11759616 | tf_op jit(solution)/shard_map/bd,vd->bv/dot_general | solution.py:100
  354.0 1.0 exponential_reduce_fusion
  355.0 28.1 %all-gather.1 = f32[32,2,1024]{2,1,0:T(2,128)S(1)} all-gather(f32[1,2,1024]{2,1,0:T(2,128)S(1)} %maximum_bitcast_fusion), channel_id=2, replica_groups=mesh['dp'=1,'yax'=4,'xax'=8] {'yax','xax'}, dimensions={0}, use_global_device_ids=true | all-gather | bytes 270336 | tf_op jit(solution)/shard_map/all_gather | solution.py:103
  383.1 0.2 fusion.45
  383.3 0.1 fusion.18
  383.4 0.0 copy-start.6
  383.4 3.5 broadcast_subtract_fusion
  (34 shorter events, 0.2 us)
Async XLA Ops:
  7.2 15.5 %copy-start = (bf16[128,1024]{1,0:T(8,128)(2,1)S(1)}, bf16[128,1024]{1,0:T(8,128)(2,1)}, u32[]{:S(2)}) copy-start(bf16[128,1024]{1,0:T(8,128)(2,1)} %param.23) | copy-start | bytes 786436
  7.2 23.1 %copy-start.3 = (bf16[1024,128]{1,0:T(8,128)(2,1)S(1)}, bf16[1024,128]{1,0:T(8,128)(2,1)}, u32[]{:S(2)}) copy-start(bf16[1024,128]{1,0:T(8,128)(2,1)} %param.14) | copy-start | bytes 786436
  7.2 23.1 %copy-start.9 = (f32[128]{0:T(128)S(1)}, f32[128]{0:T(128)}, u32[]{:S(2)}) copy-start(f32[128]{0:T(128)} %param.18) | copy-start | bytes 1540
  7.2 23.1 %copy-start.4 = (bf16[128,256]{1,0:T(8,128)(2,1)S(1)}, bf16[128,256]{1,0:T(8,128)(2,1)}, u32[]{:S(2)}) copy-start(bf16[128,256]{1,0:T(8,128)(2,1)} %param.19) | copy-start | bytes 196612
  7.2 23.5 %copy-start.7 = (bf16[128,64]{0,1:T(8,128)(2,1)S(1)}, bf16[128,64]{0,1:T(8,128)(2,1)}, u32[]{:S(2)}) copy-start(bf16[128,64]{0,1:T(8,128)(2,1)} %param.21) | copy-start | bytes 49156
  7.2 24.0 %copy-start.8 = (bf16[128,64]{0,1:T(8,128)(2,1)S(1)}, bf16[128,64]{0,1:T(8,128)(2,1)}, u32[]{:S(2)}) copy-start(bf16[128,64]{0,1:T(8,128)(2,1)} %param.20) | copy-start | bytes 49156
  42.1 110.6 %copy-start.11 = (s32[1024]{0:T(1024)S(1)}, s32[1024]{0:T(1024)}, u32[]{:S(2)}) copy-start(s32[1024]{0:T(1024)} %param.15) | copy-start | bytes 12292
  158.2 13.5 %all-to-all-start = ((bf16[4,2,32768]{2,1,0:T(2,128)(2,1)}), bf16[4,2,32768]{2,1,0:T(2,128)(2,1)S(1)}, u32[]{:S(2)}, u32[]{:S(2)}) async-start(bf16[4,2,32768]{2,1,0:T(2,128)(2,1)} %reshape.163), calls=%async_computation | async-start | bytes 1048576 | tf_op jit(solution)/shard_map/all_to_all | solution.py:85
  165.4 14.8 %copy-start.10 = (bf16[32,64]{1,0:T(8,128)(2,1)}, bf16[32,64]{1,0:T(8,128)(2,1)S(1)}, u32[]{:S(2)}) copy-start(bf16[32,64]{1,0:T(8,128)(2,1)S(1)} %get-tuple-element.45) | copy-start | bytes 12292
  180.2 3.2 copy-start.2
  186.0 36.4 %copy-start.13 = (bf16[1024,128]{1,0:T(8,128)(2,1)S(1)}, bf16[1024,128]{1,0:T(8,128)(2,1)}, u32[]{:S(2)}) copy-start(bf16[1024,128]{1,0:T(8,128)(2,1)} %param.25) | copy-start | bytes 786436
  218.7 10.2 %all-to-all-start.1 = ((bf16[256,16,64]{0,2,1:T(8,128)(2,1)}), bf16[256,16,64]{0,2,1:T(8,128)(2,1)S(1)}, u32[]{:S(2)}, u32[]{:S(2)}) async-start(bf16[256,16,64]{0,2,1:T(8,128)(2,1)} %copy.62), calls=%async_computation.1 | async-start | bytes 1048576 | tf_op jit(solution)/shard_map/all_to_all | solution.py:92
  222.3 7.1 %copy-start.5 = (bf16[256,128]{1,0:T(8,128)(2,1)S(1)}, bf16[256,128]{1,0:T(8,128)(2,1)}, u32[]{:S(2)}) copy-start(bf16[256,128]{1,0:T(8,128)(2,1)} %param.24) | copy-start | bytes 196612
  222.3 64.9 %copy-start.12 = (f32[128]{0:T(128)S(1)}, f32[128]{0:T(128)}, u32[]{:S(2)}) copy-start(f32[128]{0:T(128)} %param.26) | copy-start | bytes 1540
  222.3 48.6 %all-reduce.3.cloned.1.call-start = ((), (), s32[]{:S(2)}) async-start(), calls=%async_computation.3 | async-start | bytes 1048576 | tf_op jit(solution)/shard_map/psum | solution.py:97
  230.7 118.1 %all-gather.4.cloned.1.call-start = ((), (), s32[]{:S(2)}) async-start(), calls=%async_computation.4 | async-start | bytes 2359296 | tf_op jit(solution)/shard_map/all_gather | solution.py:99
  383.4 3.6 copy-start.1
  383.4 3.6 copy-start.6
Sparse Core Ops, SparseCore 0:
  230.8 40.0 all-reduce.2
  289.5 37.2 all-gather.3

commit v2 on v0

v2 whole, which is shorter than its diff:
```python
import functools

import jax
import jax.numpy as jnp
import numpy as np
from jax import lax
from jax.experimental import pallas as pl
from jax.experimental.pallas import tpu as pltpu
from jax.sharding import PartitionSpec as P

EPS = 1e-6
ROPE_BASE = 10000.0
F32 = jnp.float32
BF16 = jnp.bfloat16
NT = (((1,), (1,)), ((), ()))
EMBED_CHUNKS = 8


def layer_norm(values_in, gain):
    mean = jnp.mean(values_in, axis=-1, keepdims=True)
    centred = values_in - mean
    var = jnp.mean(centred * centred, axis=-1, keepdims=True)
    return centred * lax.rsqrt(var + EPS) * gain


def row_chunks(total, count):
    tiles = total // 8
    cuts = [8 * (tiles * i // count) for i in range(count + 1)]
    return [(cuts[i], cuts[i + 1] - cuts[i]) for i in range(count)]


def kernel(cfg, lens, hidden, k_hbm, v_hbm, g_attn, g_final, w_query, w_key, w_value, w_gate, w_up,
           w_out, w_down, embed, freq,
           k_out, v_out, logits_out, norm_out,
           k_buf, v_buf, h_buf, ga_buf, gf_buf, wqt, wq_buf, gu_buf, down_buf, out_buf, kv_buf,
           n_buf, q_scr, qx_buf, q2d, snew, krep, vrep, s_scr, od_scr, o_scr, ox_buf, act, part_scr,
           rs_buf, f_buf, e_buf, e_al, z_scr, st_scr, st_buf,
           kv_sem, own_sem, z_sem, x_send, x_recv, y_send, y_recv, e_send, e_recv,
           f_send, f_recv, p_send, p_recv, s_send, s_recv):
    ys, xs, own, vocab, shift = cfg
    y = lax.axis_index("yax")
    x = lax.axis_index("xax")
    core = lax.rem(x, 2)
    partner = x + 1 - 2 * core
    blk = hidden.shape[1]
    quarter = xs * own
    head_dim = k_hbm.shape[1]
    half = head_dim // 2
    seqs = k_hbm.shape[0]
    slots = k_hbm.shape[2]
    heads = w_query.shape[1] * ys // head_dim
    groups = k_buf.shape[0]
    per = seqs // groups
    window = e_buf.shape[0]

    def lanes(i):
        return pl.ds(pl.multiple_of(i * blk, 128), blk)

    def rows(i, n):
        return pl.ds(pl.multiple_of(i * n, n), n)

    def cache_copy(g, src, dst, s):
        return pltpu.make_async_copy(src.at[pl.ds(g * per, per)], dst.at[g], kv_sem.at[s, g])

    def start_cache(g, carry):
        cache_copy(g, k_hbm, k_buf, 0).start()
        return carry
    lax.fori_loop(0, groups, start_cache, 0)

    wqt[...] = w_query[...].astype(F32).T.astype(BF16)

    barrier = pltpu.get_barrier_semaphore()

    def signal_all(i, carry):
        py = lax.rem(y + i // xs, ys)
        px = lax.rem(x + lax.rem(i, xs), xs)
        pl.semaphore_signal(barrier, inc=1, device_id={"yax": py, "xax": px},
                            device_id_type=pl.DeviceIdType.MESH)
        return carry
    lax.fori_loop(1, ys * xs, signal_all, 0)
    pl.semaphore_wait(barrier, ys * xs - 1)

    cols = wqt.shape[0] // xs
    ff = w_gate.shape[1] // xs
    x_kinds = {
        "hidden": (lambda p: hidden.at[rows(y, quarter), :], lambda s: h_buf.at[:, lanes(s)]),
        "wq": (lambda p: wqt.at[rows(p, cols), :], lambda s: wq_buf.at[y, :, lanes(s)]),
        "ga": (lambda p: g_attn, lambda s: ga_buf.at[:, lanes(s)]),
        "gf": (lambda p: g_final, lambda s: gf_buf.at[:, lanes(s)]),
        "wk": (lambda p: w_key, lambda s: kv_buf.at[pl.ds(0, head_dim), lanes(s)]),
        "wv": (lambda p: w_value, lambda s: kv_buf.at[pl.ds(head_dim, head_dim), lanes(s)]),
        "wo": (lambda p: w_out.at[rows(p, cols), :], lambda s: out_buf.at[y, :, lanes(s)]),
        "gate": (lambda p: w_gate.at[:, lanes(p)], lambda s: gu_buf.at[y, rows(s, blk), pl.ds(0, ff)]),
        "up": (lambda p: w_up.at[:, lanes(p)], lambda s: gu_buf.at[y, rows(s, blk), pl.ds(ff, ff)]),
        "down": (lambda p: w_down.at[rows(p, ff), :], lambda s: down_buf.at[y, :, lanes(s)]),
        "q": (lambda p: q_scr.at[rows(p, own), :], lambda s: qx_buf.at[s]),
        "o": (lambda p: o_scr.at[p], lambda s: ox_buf.at[rows(s, own), :]),
        "rs": (lambda p: part_scr.at[rows(p, own), :], lambda s: rs_buf.at[s]),
    }
    x_index = {name: i for i, name in enumerate(x_kinds)}

    def x_copy(name, dest, sender):
        src, dst = x_kinds[name]
        k = x_index[name]
        return pltpu.make_async_remote_copy(
            src_ref=src(dest), dst_ref=dst(sender), send_sem=x_send.at[k, dest],
            recv_sem=x_recv.at[k, sender], device_id={"xax": dest},
            device_id_type=pl.DeviceIdType.MESH)

    def own_copy(name):
        src, dst = x_kinds[name]
        return pltpu.make_async_copy(src(x), dst(x), own_sem.at[x_index[name]])

    def x_start(name):
        def body(d, carry):
            x_copy(name, lax.rem(x + d, xs), x).start()
            return carry
        lax.fori_loop(1, xs, body, 0)
        own_copy(name).start()

    def x_wait(name):
        def body(d, carry):
            x_copy(name, x, lax.rem(x + xs - d, xs)).wait_recv()
            return carry
        lax.fori_loop(1, xs, body, 0)
        own_copy(name).wait()

    def x_drain(name):
        def body(d, carry):
            x_copy(name, lax.rem(x + d, xs), x).wait_send()
            return carry
        lax.fori_loop(1, xs, body, 0)

    y_kinds = {"wq": wq_buf, "wo": out_buf, "gu": gu_buf, "down": down_buf}
    y_index = {name: i for i, name in enumerate(y_kinds)}

    def y_copy(name, dest, sender):
        buf = y_kinds[name]
        k = y_index[name]
        return pltpu.make_async_remote_copy(
            src_ref=buf.at[sender], dst_ref=buf.at[sender], send_sem=y_send.at[k, dest],
            recv_sem=y_recv.at[k, sender], device_id={"yax": dest},
            device_id_type=pl.DeviceIdType.MESH)

    def y_start(name):
        def body(d, carry):
            y_copy(name, lax.rem(y + d, ys), y).start()
            return carry
        lax.fori_loop(1, ys, body, 0)

    def y_wait(name):
        def body(d, carry):
            y_copy(name, y, lax.rem(y + ys - d, ys)).wait_recv()
            return carry
        lax.fori_loop(1, ys, body, 0)

    def y_drain(name):
        def body(d, carry):
            y_copy(name, lax.rem(y + d, ys), y).wait_send()
            return carry
        lax.fori_loop(1, ys, body, 0)

    e_parts = row_chunks(window, EMBED_CHUNKS)

    def e_first(p):
        return p * vocab - lax.rem(p, 2) * shift

    def e_copy(c, dest, sender):
        r0, n = e_parts[c]
        return pltpu.make_async_remote_copy(
            src_ref=embed.at[pl.ds(pl.multiple_of(e_first(dest) + r0, 8), n), :],
            dst_ref=e_buf.at[pl.ds(r0, n), lanes(sender)],
            send_sem=e_send.at[c, dest], recv_sem=e_recv.at[c, sender],
            device_id={"xax": dest}, device_id_type=pl.DeviceIdType.MESH)

    def e_own():
        return pltpu.make_async_copy(
            embed.at[pl.ds(pl.multiple_of(e_first(x), 8), window), :], e_buf.at[:, lanes(x)],
            own_sem.at[len(x_kinds)])

    def e_start(c):
        def body(d, carry):
            e_copy(c, lax.rem(x + d, xs), x).start()
            return carry
        lax.fori_loop(1, xs, body, 0)

    for name in ("hidden", "wq", "ga", "gf", "wk", "wv", "wo", "gate", "up", "down"):
        x_start(name)
    e_own().start()

    def start_cache_v(g, carry):
        cache_copy(g, v_hbm, v_buf, 1).start()
        return carry
    lax.fori_loop(0, groups, start_cache_v, 0)
    e_start(0)

    x_wait("wq")
    y_start("wq")
    x_wait("hidden")
    x_wait("ga")
    n_buf[...] = layer_norm(h_buf[...].astype(F32), ga_buf[...]).astype(BF16)
    y_wait("wq")
    wq_all = wq_buf[...].reshape(ys * cols, xs * blk)
    q_scr[...] = lax.dot_general(n_buf[...], wq_all, NT, preferred_element_type=F32).astype(BF16)
    x_start("q")
    x_wait("wo")
    y_start("wo")
    x_wait("gate")
    x_wait("up")
    y_start("gu")
    x_wait("down")
    y_start("down")
    e_start(1)

    row_id = lax.broadcasted_iota(jnp.int32, (own, 4 * half), 0)
    first_row = (y * xs + x) * own
    position = jnp.zeros((own, 4 * half), jnp.int32)
    for b in range(own):
        position = jnp.where(row_id == b, lens[first_row + b], position)
    angle = position.astype(F32) * freq[...]
    cos_a = jnp.cos(angle)
    sin_a = jnp.sin(angle)
    x_wait("wk")
    x_wait("wv")
    n_own = n_buf[rows(x, own), :]
    kv = lax.dot_general(n_own, kv_buf[...], NT, preferred_element_type=F32).astype(BF16).astype(F32)
    k1 = kv[:, :half]
    k2 = kv[:, half:head_dim]
    c1 = cos_a[:, :half]
    s1 = sin_a[:, :half]
    key = jnp.concatenate([k1 * c1 - k2 * s1, k2 * c1 + k1 * s1], axis=1).astype(BF16)
    value = kv[:, head_dim:].astype(BF16)
    k_out[...] = key
    v_out[...] = value
    for h in range(heads):
        krep[pl.ds(h, own, stride=heads), :] = key.astype(F32)
        vrep[pl.ds(h, own, stride=heads), :] = value.astype(F32)

    x_wait("q")
    for xc in range(xs // 2):
        qa = qx_buf[2 * xc].astype(F32)
        qb = qx_buf[2 * xc + 1].astype(F32)
        ra = (qa * cos_a - qb * sin_a).astype(BF16).astype(F32)
        rb = (qb * cos_a + qa * sin_a).astype(BF16).astype(F32)
        for yc in range(ys):
            pair = jnp.concatenate([ra[:, yc * half:(yc + 1) * half], rb[:, yc * half:(yc + 1) * half]], axis=1)
            q2d[pl.ds(xc * ys + yc, own, stride=heads), :] = pair
    scale = head_dim ** -0.5
    snew[...] = jnp.sum(q2d[...] * krep[...], axis=1, keepdims=True) * scale

    gr = per * heads
    seg_r = lax.broadcasted_iota(jnp.int32, (gr, per * head_dim), 0) // heads
    seg_c = lax.broadcasted_iota(jnp.int32, (gr, per * head_dim), 1) // head_dim
    diag = (seg_r == seg_c).astype(F32)
    tile = min(512, slots)
    row_g = lax.broadcasted_iota(jnp.int32, (gr, 1), 0) // heads
    lane_g = lax.broadcasted_iota(jnp.int32, (gr, tile), 1)

    def attend(g, carry):
        cache_copy(g, k_hbm, k_buf, 0).wait()
        qg = q2d[rows(g, gr), :]
        qbd = (jnp.concatenate([qg] * per, axis=1) * diag).astype(BF16)
        len_g = jnp.zeros((gr, 1), jnp.int32)
        for s in range(per):
            len_g = jnp.where(row_g == s, lens[first_row + g * per + s], len_g)
        new = snew[rows(g, gr), :]
        top = jnp.full((gr, tile), -jnp.inf, F32)
        kg = k_buf.at[g]
        vg = v_buf.at[g]
        for c in range(slots // tile):
            kc = kg[:, :, pl.ds(c * tile, tile)].reshape(per * head_dim, tile)
            sc = jnp.dot(qbd, kc, preferred_element_type=F32) * scale
            sc = jnp.where(lane_g < len_g - c * tile, sc, -jnp.inf)
            s_scr[:, pl.ds(c * tile, tile)] = sc
            top = jnp.maximum(top, sc)
        row_max = jnp.maximum(jnp.max(top, axis=1, keepdims=True), new)
        total = jnp.zeros((gr, tile), F32)
        for c in range(slots // tile):
            ex = jnp.exp(s_scr[:, pl.ds(c * tile, tile)] - row_max)
            s_scr[:, pl.ds(c * tile, tile)] = ex
            total = total + ex
        w_new = jnp.exp(new - row_max)
        den = jnp.sum(total, axis=1, keepdims=True) + w_new
        inv = 1.0 / den
        cache_copy(g, v_hbm, v_buf, 1).wait()
        mixed = jnp.zeros((gr, per * head_dim), F32)
        for c in range(slots // tile):
            pr = (s_scr[:, pl.ds(c * tile, tile)] * inv).astype(BF16)
            vc = vg[:, :, pl.ds(c * tile, tile)].reshape(per * head_dim, tile)
            mixed = mixed + lax.dot_general(pr, vc, NT, preferred_element_type=F32)
        add = (w_new * inv).astype(BF16).astype(F32) * vrep[rows(g, gr), :]
        for s in range(per):
            od_scr[pl.ds(pl.multiple_of(g * gr + s * heads, heads), heads), :] = (
                mixed[s * heads:(s + 1) * heads, s * head_dim:(s + 1) * head_dim]
                + add[s * heads:(s + 1) * heads, :])
        return carry

    e_done = 2
    steps = 4
    for i in range(steps):
        lax.fori_loop(i * groups // steps, (i + 1) * groups // steps, attend, 0)
        if e_done < EMBED_CHUNKS:
            e_start(e_done)
            e_done += 1
    for xc in range(xs // 2):
        parts = [od_scr[pl.ds(xc * ys + yc, own, stride=heads), :] for yc in range(ys)]
        o_scr[2 * xc] = jnp.concatenate([p[:, :half] for p in parts], axis=1).astype(BF16)
        o_scr[2 * xc + 1] = jnp.concatenate([p[:, half:] for p in parts], axis=1).astype(BF16)
    x_start("o")

    y_wait("gu")
    for j in range(ys):
        gu = jnp.dot(n_buf[...], gu_buf[j], preferred_element_type=F32).astype(BF16).astype(F32)
        gate = gu[:, :ff]
        act[:, pl.ds(j * ff, ff)] = (gate * jax.nn.sigmoid(gate) * gu[:, ff:]).astype(BF16)
    y_wait("down")
    part_scr[...] = jnp.dot(act[...], down_buf[...].reshape(ys * ff, xs * blk), preferred_element_type=F32)
    y_wait("wo")
    x_wait("o")
    part_scr[...] = part_scr[...] + jnp.dot(
        ox_buf[...], out_buf[...].reshape(ys * cols, xs * blk), preferred_element_type=F32)
    x_start("rs")
    while e_done < EMBED_CHUNKS:
        e_start(e_done)
        e_done += 1
    x_wait("gf")
    x_wait("rs")
    res = h_buf[rows(x, own), :].astype(F32) + jnp.sum(rs_buf[...], axis=0)
    mine = y * xs + x
    f_buf[rows(mine, own), :] = layer_norm(res, gf_buf[...]).astype(BF16)

    chips = xs // 2

    def f_copy(dy, dx, src_y, src_x):
        r = rows(src_y * xs + src_x, own)
        return pltpu.make_async_remote_copy(
            src_ref=f_buf.at[r, :], dst_ref=f_buf.at[r, :],
            send_sem=f_send.at[dy * xs + dx], recv_sem=f_recv.at[src_y * xs + src_x],
            device_id={"yax": dy, "xax": dx}, device_id_type=pl.DeviceIdType.MESH)

    def p_copy(src_y, src_x):
        r = rows(src_y * xs + src_x, own)
        return pltpu.make_async_remote_copy(
            src_ref=f_buf.at[r, :], dst_ref=f_buf.at[r, :],
            send_sem=p_send.at[src_y * xs + src_x], recv_sem=p_recv.at[src_y * xs + src_x],
            device_id={"xax": partner}, device_id_type=pl.DeviceIdType.MESH)

    def plane_peer(i, sign):
        py = lax.rem(y + ys + sign * (i // chips), ys)
        px = lax.rem(x + xs + sign * 2 * lax.rem(i, chips), xs)
        return py, px

    def f_start(i, carry):
        py, px = plane_peer(i, 1)
        f_copy(py, px, y, x).start()
        return carry
    lax.fori_loop(1, ys * chips, f_start, 0)
    p_copy(y, x).start()

    e_own().wait()
    for c in range(EMBED_CHUNKS):
        def e_wait(d, carry, c=c):
            e_copy(c, x, lax.rem(x + xs - d, xs)).wait_recv()
            return carry
        lax.fori_loop(1, xs, e_wait, 0)
    if shift:
        @pl.when(core == 1)
        def _():
            for r0 in range(0, vocab, 256):
                n = min(256, vocab - r0)
                e_al[pl.ds(r0, n), :] = e_buf[pl.ds(r0 + shift, n), :]

        @pl.when(core == 0)
        def _():
            for r0 in range(0, vocab, 256):
                n = min(256, vocab - r0)
                e_al[pl.ds(r0, n), :] = e_buf[pl.ds(r0, n), :]
    else:
        e_al[...] = e_buf[...]

    def z_copy(j, slot):
        return pltpu.make_async_copy(z_scr.at[slot], logits_out.at[:, rows(j, quarter)], z_sem.at[slot])

    def head(dy, carry):
        j = lax.rem(y + ys - dy, ys)

        def forward(i, c2):
            sx = lax.rem(x + xs - 2 * i, xs)

            @pl.when(jnp.logical_or(dy > 0, i > 0))
            def _():
                f_copy(y, x, j, sx).wait_recv()
                p_copy(j, sx).start()
            return c2
        lax.fori_loop(0, chips, forward, 0)

        def arrive(i, c2):
            p_copy(j, lax.rem(partner + xs - 2 * i, xs)).wait_recv()
            return c2
        lax.fori_loop(0, chips, arrive, 0)
        slot = lax.rem(dy, 2)

        @pl.when(dy >= 2)
        def _():
            z_copy(j, slot).wait()
        z = lax.dot_general(e_al[...], f_buf[rows(j, quarter), :], NT, preferred_element_type=F32)
        z_scr[slot] = z
        z_copy(j, slot).start()
        top = jnp.max(z, axis=0, keepdims=True)
        tot = jnp.sum(jnp.exp(z - top), axis=0, keepdims=True)
        st_scr[0:1, rows(j, quarter)] = top
        st_scr[1:2, rows(j, quarter)] = tot
        return carry
    lax.fori_loop(0, ys, head, 0)

    def s_copy(dest_y, dest_x, src):
        return pltpu.make_async_remote_copy(
            src_ref=st_scr, dst_ref=st_buf.at[src], send_sem=s_send.at[dest_y * xs + dest_x],
            recv_sem=s_recv.at[src], device_id={"yax": dest_y, "xax": dest_x},
            device_id_type=pl.DeviceIdType.MESH)

    def s_start(i, carry):
        s_copy(lax.rem(y + i // xs, ys), lax.rem(x + lax.rem(i, xs), xs), mine).start()
        return carry
    lax.fori_loop(1, ys * xs, s_start, 0)
    st_buf[mine] = st_scr[...]

    for name in x_kinds:
        x_drain(name)
    for name in y_kinds:
        y_drain(name)
    for c in range(EMBED_CHUNKS):
        def e_drain(d, carry, c=c):
            e_copy(c, lax.rem(x + d, xs), x).wait_send()
            return carry
        lax.fori_loop(1, xs, e_drain, 0)

    def f_drain(i, carry):
        py, px = plane_peer(i, 1)
        f_copy(py, px, y, x).wait_send()
        return carry
    lax.fori_loop(1, ys * chips, f_drain, 0)

    def p_drain(i, carry):
        py, px = plane_peer(i, 1)
        p_copy(py, px).wait_send()
        return carry
    lax.fori_loop(0, ys * chips, p_drain, 0)

    def s_wait(i, carry):
        sy = lax.rem(y + ys - i // xs, ys)
        sx = lax.rem(x + xs - lax.rem(i, xs), xs)
        s_copy(y, x, sy * xs + sx).wait_recv()
        return carry
    lax.fori_loop(1, ys * xs, s_wait, 0)
    tops = st_buf[:, 0, :]
    best = jnp.max(tops, axis=0, keepdims=True)
    whole = jnp.sum(st_buf[:, 1, :] * jnp.exp(tops - best), axis=0, keepdims=True)
    norm_out[...] = best + jnp.log(whole)

    def s_drain(i, carry):
        s_copy(lax.rem(y + i // xs, ys), lax.rem(x + lax.rem(i, xs), xs), mine).wait_send()
        return carry
    lax.fori_loop(1, ys * xs, s_drain, 0)
    for dy in range(max(ys - 2, 0), ys):
        z_copy(lax.rem(y + ys - dy, ys), dy % 2).wait()


def solution(mesh):
    ys = mesh.shape["yax"]
    xs = mesh.shape["xax"]
    row_spec = P(("dp", "yax", "xax"))

    def local_step(hidden, cache_len, k_cache, v_cache, g_attn, w_query, w_key, w_value,
                   w_gate, w_up, w_out, w_down, g_final, embedding):
        batch, blk = hidden.shape
        own, slots, head_dim = k_cache.shape
        width = blk * xs
        vocab = embedding.shape[0] // xs
        shift = vocab % 8
        window = -(-vocab // 8) * 8
        half = head_dim // 2
        quarter = xs * own
        cols = w_query.shape[1] // xs
        ff = w_gate.shape[1] // xs
        heads = w_query.shape[1] * ys // head_dim
        per = 4
        groups = own // per
        freq_row = (ROPE_BASE ** (-(np.arange(half, dtype=np.float32) * 2.0) / head_dim)).astype(np.float32)
        freq = jnp.asarray(np.tile(freq_row, 4)[None, :])
        any_spec = pl.BlockSpec(memory_space=pl.ANY)
        vmem = pl.BlockSpec(memory_space=pltpu.VMEM)
        smem = pl.BlockSpec(memory_space=pltpu.SMEM)
        dma = pltpu.SemaphoreType.DMA
        nx = 13
        all_n = ys * xs
        scratch = [
            pltpu.VMEM((groups, per, head_dim, slots), BF16),
            pltpu.VMEM((groups, per, head_dim, slots), BF16),
            pltpu.VMEM((quarter, width), BF16),
            pltpu.VMEM((1, width), F32),
            pltpu.VMEM((1, width), F32),
            pltpu.VMEM((w_query.shape[1], blk), BF16),
            pltpu.VMEM((ys, cols, width), BF16),
            pltpu.VMEM((ys, width, 2 * ff), BF16),
            pltpu.VMEM((ys, ff, width), BF16),
            pltpu.VMEM((ys, cols, width), BF16),
            pltpu.VMEM((2 * head_dim, width), BF16),
            pltpu.VMEM((quarter, width), BF16),
            pltpu.VMEM((quarter, ys * cols), BF16),
            pltpu.VMEM((xs, own, ys * cols), BF16),
            pltpu.VMEM((own * heads, head_dim), F32),
            pltpu.VMEM((own * heads, 1), F32),
            pltpu.VMEM((own * heads, head_dim), F32),
            pltpu.VMEM((own * heads, head_dim), F32),
            pltpu.VMEM((per * heads, slots), F32),
            pltpu.VMEM((own * heads, head_dim), F32),
            pltpu.VMEM((xs, own, ys * cols), BF16),
            pltpu.VMEM((quarter, ys * cols), BF16),
            pltpu.VMEM((quarter, ys * ff), BF16),
            pltpu.VMEM((quarter, width), F32),
            pltpu.VMEM((xs, own, width), F32),
            pltpu.VMEM((batch, width), BF16),
            pltpu.VMEM((window, width), BF16),
            pltpu.VMEM((vocab, width), BF16),
            pltpu.VMEM((2, vocab, quarter), F32),
            pltpu.VMEM((2, batch), F32),
            pltpu.VMEM((all_n, 2, batch), F32),
            dma((2, groups)), dma((nx + 1,)), dma((2,)),
            dma((nx, xs)), dma((nx, xs)), dma((4, ys)), dma((4, ys)),
            dma((EMBED_CHUNKS, xs)), dma((EMBED_CHUNKS, xs)),
            dma((all_n,)), dma((all_n,)), dma((all_n,)), dma((all_n,)), dma((all_n,)), dma((all_n,)),
        ]
        cfg = (ys, xs, own, vocab, shift)
        key_new, value_new, logits, norm = pl.pallas_call(
            functools.partial(kernel, cfg),
            name="decode_layer",
            out_shape=(
                jax.ShapeDtypeStruct((own, head_dim), BF16),
                jax.ShapeDtypeStruct((own, head_dim), BF16),
                jax.ShapeDtypeStruct((vocab, batch), F32),
                jax.ShapeDtypeStruct((1, batch), F32)),
            in_specs=[smem, any_spec, any_spec, any_spec, any_spec, any_spec, vmem] + [any_spec] * 7 + [vmem],
            out_specs=(vmem, vmem, any_spec, vmem),
            scratch_shapes=scratch,
            compiler_params=pltpu.CompilerParams(
                collective_id=0, has_side_effects=True, vmem_limit_bytes=67043328),
        )(cache_len, hidden, k_cache.transpose(0, 2, 1), v_cache.transpose(0, 2, 1),
          g_attn[None, :], g_final[None, :], w_query, w_key.T, w_value.T, w_gate, w_up, w_out, w_down,
          embedding, freq)
        log_norm = norm[0]
        return key_new, value_new, (logits - norm).T, log_norm

    in_specs = (P("dp", "xax"), P("dp"), row_spec, row_spec, P("xax"), P("xax", "yax"),
                P("xax", None), P("xax", None), P("xax", "yax"), P("xax", "yax"),
                P("yax", "xax"), P("yax", "xax"), P("xax"), P("yax", "xax"))
    out_specs = (row_spec, row_spec, P("dp", ("yax", "xax")), P("dp"))
    return jax.shard_map(local_step, mesh=mesh, in_specs=in_specs, out_specs=out_specs, check_vma=False)
```

time: 771 us -> 127 us (0.16)
  blocking collectives: 540 us -> 0 us
  Pallas kernels: 0 us -> 118 us
  matrix products: 59.3 us -> 0 us
  local copies, waits for them, and re-layouts: 55.3 us -> 1.8 us
  waiting for transfers between devices: 51.1 us -> 0 us
  other arithmetic: 33.4 us -> 6.44 us
  between operations: 15 us -> 0.67 us
  starting transfers between devices: 14.3 us -> 0 us
    unnamed x1 -> x0, blocking collectives: 295 us -> none
    psum x4 -> x0, blocking collectives: 180 us -> none  [the longest x1 108 us: local_step(): projected = lax.psum(proj_part, 'xax').astype(jnp.bfloat16)]
    pallas_call x0 -> x1, Pallas kernels: none -> 118 us  [local_step(): pl.pallas_call(functools.partial(kernel, cfg), name='decode_layer', out_s...]
    dot_general x11 -> x0, matrix products: 59.3 us -> none  [the longest x1 21 us: local_step(): jnp.einsum('bd,vd->bv', final_norm, embedding, preferred_element_type=jnp...]
    pmax x1 -> x0, blocking collectives: 44.6 us -> none  [local_step(): row_max = lax.pmax(jnp.max(logits, axis=1), ('yax', 'xax'))]
    psum x1 -> x0, waiting for transfers between devices: 40.3 us -> none  [local_step(): residual_out = residual + lax.psum(branch_sum, 'yax')]
    unnamed x30 -> x9, local copies, waits for them, and re-layouts: 29.8 us -> 1.8 us
    all_gather x1 -> x0, blocking collectives: 20.4 us -> none  [local_step(): attn_grp = lax.all_gather(attn_own, 'xax', axis=0, tiled=True)]
  transfers between devices with their start and end apart: 4 -> 0, of which waited for: 4 -> 0; matrix products, arithmetic and copies ran while one was open for 1% -> 0% of each run, Pallas kernels for 0% -> 0%
where the time goes in v2:
time: 127 us
  Pallas kernels  118 us (93%)
  other arithmetic  6.44 us (5%)
  local copies, waits for them, and re-layouts  1.8 us (1%)
    pallas_call x1, Pallas kernels, local_step(): pl.pallas_call(functools.partial(kernel, cfg), name='decode_layer', out_s...  118 us
    transpose x1, other arithmetic, local_step(): return (key_new, value_new, (logits - norm).T, log_norm)  6.44 us

profile of v2, /device:TPU:97, one launch (start us, length us, event | category | flops | bytes accessed | tf_op | source)
XLA Modules:
  0.0 126.8 jit_solution(15091846451653141317)
XLA Ops:
  0.6 117.8 %decode_layer.1 = (bf16[32,64]{1,0:T(8,128)(2,1)}, bf16[32,64]{1,0:T(8,128)(2,1)}, f32[1572,1024]{1,0:T(8,128)}, f32[1,1024]{1,0:T(1,128)}) custom-call(s32[1024]{0:T(1024)} %lens.1, bf16[1024,128]{1,0:T(8,128)(2,1)} %hidden.1, bf16[32,64,4096]{2,1,0:T(8,128)(2,1)} %bitcast.9, bf16[32,64,4096]{2,1,0:T(8,128)(2,1)} %bitcast.10, f32[1,128]{1,0:T(1,128)} %bitcast.15, ...), custom_call_target="tpu_custom_call" | custom-call | tf_op jit(solution)/shard_map/decode_layer/pallas_call | solution.py:535
  118.5 0.0 copy-start.2
  118.5 0.0 copy-start.1
  118.5 0.0 copy-start
  118.5 6.4 %subtract_bitcast_fusion = f32[1024,1572]{0,1:T(8,128)} fusion(f32[1572,1024]{1,0:T(8,128)} %get-tuple-element.10, f32[1024]{0:T(1024)} %bitcast.13), kind=kLoop, calls=%fused_computation | loop fusion | flops 1609728 | bytes 12881920 | tf_op jit(solution)/shard_map/transpose | solution.py:552
  125.0 0.0 copy-done.2
  125.0 0.6 copy.22
  125.6 0.0 copy-done.1
  125.6 0.6 copy.23
  126.2 0.0 copy-done
  126.2 0.6 copy.24
Async XLA Ops:
  118.5 6.5 %copy-start.2 = (bf16[32,64]{1,0:T(8,128)(2,1)S(1)}, bf16[32,64]{1,0:T(8,128)(2,1)}, u32[]{:S(2)}) copy-start(bf16[32,64]{1,0:T(8,128)(2,1)} %get-tuple-element.16) | copy-start | bytes 12292
  118.5 7.1 %copy-start.1 = (bf16[32,64]{1,0:T(8,128)(2,1)S(1)}, bf16[32,64]{1,0:T(8,128)(2,1)}, u32[]{:S(2)}) copy-start(bf16[32,64]{1,0:T(8,128)(2,1)} %get-tuple-element.17) | copy-start | bytes 12292
  118.5 7.7 %copy-start = (f32[1,1024]{1,0:T(1,128)S(1)}, f32[1,1024]{1,0:T(1,128)}, u32[]{:S(2)}) copy-start(f32[1,1024]{1,0:T(1,128)} %get-tuple-element.11) | copy-start | bytes 12292

commit v3 on v2

--- a/solution.py
+++ b/solution.py
@@ -33,10 +33,10 @@
            w_out, w_down, embed, freq,
            k_out, v_out, logits_out, norm_out,
            k_buf, v_buf, h_buf, ga_buf, gf_buf, wqt, wq_buf, gu_buf, down_buf, out_buf, kv_buf,
-           n_buf, q_scr, qx_buf, q2d, snew, krep, vrep, s_scr, od_scr, o_scr, ox_buf, act, part_scr,
-           rs_buf, f_buf, e_buf, e_al, z_scr, st_scr, st_buf,
-           kv_sem, own_sem, z_sem, x_send, x_recv, y_send, y_recv, e_send, e_recv,
-           f_send, f_recv, p_send, p_recv, s_send, s_recv):
+           n_all, q_scr, qx_buf, q2d, snew, krep, vrep, s_scr, od_scr, o_scr, ox_buf, act_scr, act, part_scr,
+           pre_buf, rs_scr, rs_buf, f_buf, e_buf, e_al, z_scr, st_scr, sx_buf, sy_scr, sy_buf,
+           kv_sem, own_sem, z_sem, x_send, x_recv, g_send, y_send, y_recv, e_send, e_recv,
+           n_recv, n_fwd, pre_sem, f_send, f_recv, fy_send, fp_send, sx_send, sx_recv, sy_send, sy_recv):
     ys, xs, own, vocab, shift = cfg
     y = lax.axis_index("yax")
     x = lax.axis_index("xax")
@@ -71,14 +71,18 @@
 
     barrier = pltpu.get_barrier_semaphore()
 
-    def signal_all(i, carry):
-        py = lax.rem(y + i // xs, ys)
-        px = lax.rem(x + lax.rem(i, xs), xs)
-        pl.semaphore_signal(barrier, inc=1, device_id={"yax": py, "xax": px},
+    def signal_row(d, carry):
+        pl.semaphore_signal(barrier, inc=1, device_id={"xax": lax.rem(x + d, xs)},
                             device_id_type=pl.DeviceIdType.MESH)
         return carry
-    lax.fori_loop(1, ys * xs, signal_all, 0)
-    pl.semaphore_wait(barrier, ys * xs - 1)
+    lax.fori_loop(1, xs, signal_row, 0)
+
+    def signal_column(d, carry):
+        pl.semaphore_signal(barrier, inc=1, device_id={"yax": lax.rem(y + d, ys)},
+                            device_id_type=pl.DeviceIdType.MESH)
+        return carry
+    lax.fori_loop(1, ys, signal_column, 0)
+    pl.semaphore_wait(barrier, xs + ys - 2)
 
     cols = wqt.shape[0] // xs
     ff = w_gate.shape[1] // xs
@@ -90,12 +94,11 @@
         "wk": (lambda p: w_key, lambda s: kv_buf.at[pl.ds(0, head_dim), lanes(s)]),
         "wv": (lambda p: w_value, lambda s: kv_buf.at[pl.ds(head_dim, head_dim), lanes(s)]),
         "wo": (lambda p: w_out.at[rows(p, cols), :], lambda s: out_buf.at[y, :, lanes(s)]),
-        "gate": (lambda p: w_gate.at[:, lanes(p)], lambda s: gu_buf.at[y, rows(s, blk), pl.ds(0, ff)]),
-        "up": (lambda p: w_up.at[:, lanes(p)], lambda s: gu_buf.at[y, rows(s, blk), pl.ds(ff, ff)]),
+        "gate": (lambda p: w_gate.at[:, lanes(p)], lambda s: gu_buf.at[rows(s, blk), pl.ds(0, ff)]),
+        "up": (lambda p: w_up.at[:, lanes(p)], lambda s: gu_buf.at[rows(s, blk), pl.ds(ff, ff)]),
         "down": (lambda p: w_down.at[rows(p, ff), :], lambda s: down_buf.at[y, :, lanes(s)]),
         "q": (lambda p: q_scr.at[rows(p, own), :], lambda s: qx_buf.at[s]),
         "o": (lambda p: o_scr.at[p], lambda s: ox_buf.at[rows(s, own), :]),
-        "rs": (lambda p: part_scr.at[rows(p, own), :], lambda s: rs_buf.at[s]),
     }
     x_index = {name: i for i, name in enumerate(x_kinds)}
 
@@ -111,6 +114,50 @@
         src, dst = x_kinds[name]
         return pltpu.make_async_copy(src(x), dst(x), own_sem.at[x_index[name]])
 
+    chips = xs // 2
+    gathers = {name: i for i, name in enumerate(("hidden", "ga", "gf", "wk", "wv"))}
+
+    def g_copy(name, sender, source):
+        src, dst = x_kinds[name]
+        return pltpu.make_async_remote_copy(
+            src_ref=source, dst_ref=dst(sender), send_sem=g_send.at[gathers[name], sender],
+            recv_sem=x_recv.at[x_index[name], sender], device_id={"xax": partner},
+            device_id_type=pl.DeviceIdType.MESH)
+
+    def g_start(name):
+        def body(i, carry):
+            x_copy(name, lax.rem(x + 2 * i, xs), x).start()
+            return carry
+        lax.fori_loop(1, chips, body, 0)
+        g_copy(name, x, x_kinds[name][0](x)).start()
+        own_copy(name).start()
+
+    def g_forward(name):
+        def body(i, carry):
+            sender = lax.rem(x + xs - 2 * i, xs)
+            x_copy(name, x, sender).wait_recv()
+            g_copy(name, sender, x_kinds[name][1](sender)).start()
+            return carry
+        lax.fori_loop(1, chips, body, 0)
+
+    def g_wait(name):
+        def body(i, carry):
+            sender = lax.rem(partner + xs - 2 * i, xs)
+            g_copy(name, sender, x_kinds[name][1](sender)).wait_recv()
+            return carry
+        lax.fori_loop(0, chips, body, 0)
+        own_copy(name).wait()
+
+    def g_drain(name):
+        def body(i, carry):
+            @pl.when(i > 0)
+            def _():
+                x_copy(name, lax.rem(x + 2 * i, xs), x).wait_send()
+            sender = lax.rem(x + xs - 2 * i, xs)
+            g_copy(name, sender, x_kinds[name][1](sender)).wait_send()
+            return carry
+        lax.fori_loop(0, chips, body, 0)
+
     def x_start(name):
         def body(d, carry):
             x_copy(name, lax.rem(x + d, xs), x).start()
@@ -131,7 +178,7 @@
             return carry
         lax.fori_loop(1, xs, body, 0)
 
-    y_kinds = {"wq": wq_buf, "wo": out_buf, "gu": gu_buf, "down": down_buf}
+    y_kinds = {"wq": wq_buf, "wo": out_buf, "down": down_buf}
     y_index = {name: i for i, name in enumerate(y_kinds)}
 
     def y_copy(name, dest, sender):
@@ -184,33 +231,64 @@
             return carry
         lax.fori_loop(1, xs, body, 0)
 
-    for name in ("hidden", "wq", "ga", "gf", "wk", "wv", "wo", "gate", "up", "down"):
+    x_start("wq")
+    for name in ("hidden", "ga"):
+        g_start(name)
+    for name in ("wo", "down"):
         x_start(name)
+    for name in ("wk", "wv", "gf"):
+        g_start(name)
     e_own().start()
 
     def start_cache_v(g, carry):
         cache_copy(g, v_hbm, v_buf, 1).start()
         return carry
     lax.fori_loop(0, groups, start_cache_v, 0)
-    e_start(0)
 
     x_wait("wq")
     y_start("wq")
-    x_wait("hidden")
-    x_wait("ga")
-    n_buf[...] = layer_norm(h_buf[...].astype(F32), ga_buf[...]).astype(BF16)
+    for name in ("hidden", "ga"):
+        g_forward(name)
+    for name in ("hidden", "ga"):
+        g_wait(name)
+    my_rows = rows(y, quarter)
+    n_all[my_rows, :] = layer_norm(h_buf[...].astype(F32), ga_buf[...]).astype(BF16)
+
+    part = quarter // 2
+
+    def n_rows(j, c):
+        return pl.ds(pl.multiple_of(j * quarter + c * part, part), part)
+
+    def n_copy(dest, sender):
+        r = n_rows(sender, core)
+        return pltpu.make_async_remote_copy(
+            src_ref=n_all.at[r, :], dst_ref=n_all.at[r, :], send_sem=y_send.at[len(y_kinds), dest],
+            recv_sem=n_recv.at[sender, core], device_id={"yax": dest},
+            device_id_type=pl.DeviceIdType.MESH)
+
+    def n_pass(sender, c):
+        r = n_rows(sender, c)
+        return pltpu.make_async_remote_copy(
+            src_ref=n_all.at[r, :], dst_ref=n_all.at[r, :], send_sem=n_fwd.at[sender],
+            recv_sem=n_recv.at[sender, c], device_id={"xax": partner},
+            device_id_type=pl.DeviceIdType.MESH)
+
     y_wait("wq")
     wq_all = wq_buf[...].reshape(ys * cols, xs * blk)
-    q_scr[...] = lax.dot_general(n_buf[...], wq_all, NT, preferred_element_type=F32).astype(BF16)
+    q_scr[...] = lax.dot_general(n_all[my_rows, :], wq_all, NT, preferred_element_type=F32).astype(BF16)
     x_start("q")
+    x_start("gate")
+    x_start("up")
+
+    def n_start(d, carry):
+        n_copy(lax.rem(y + d, ys), y).start()
+        return carry
+    lax.fori_loop(1, ys, n_start, 0)
     x_wait("wo")
     y_start("wo")
-    x_wait("gate")
-    x_wait("up")
-    y_start("gu")
     x_wait("down")
     y_start("down")
-    e_start(1)
+    e_start(0)
 
     row_id = lax.broadcasted_iota(jnp.int32, (own, 4 * half), 0)
     first_row = (y * xs + x) * own
@@ -220,9 +298,12 @@
     angle = position.astype(F32) * freq[...]
     cos_a = jnp.cos(angle)
     sin_a = jnp.sin(angle)
-    x_wait("wk")
-    x_wait("wv")
-    n_own = n_buf[rows(x, own), :]
+    for name in ("wk", "wv", "gf"):
+        g_forward(name)
+    for name in ("wk", "wv", "gf"):
+        g_wait(name)
+    mine = y * xs + x
+    n_own = n_all[rows(mine, own), :]
     kv = lax.dot_general(n_own, kv_buf[...], NT, preferred_element_type=F32).astype(BF16).astype(F32)
     k1 = kv[:, :half]
     k2 = kv[:, half:head_dim]
@@ -295,7 +376,7 @@
                 + add[s * heads:(s + 1) * heads, :])
         return carry
 
-    e_done = 2
+    e_done = 1
     steps = 4
     for i in range(steps):
         lax.fori_loop(i * groups // steps, (i + 1) * groups // steps, attend, 0)
@@ -308,54 +389,135 @@
         o_scr[2 * xc + 1] = jnp.concatenate([p[:, half:] for p in parts], axis=1).astype(BF16)
     x_start("o")
 
-    y_wait("gu")
-    for j in range(ys):
-        gu = jnp.dot(n_buf[...], gu_buf[j], preferred_element_type=F32).astype(BF16).astype(F32)
+    def act_copy(dest, sender):
+        return pltpu.make_async_remote_copy(
+            src_ref=act_scr.at[dest], dst_ref=act.at[:, pl.ds(pl.multiple_of(sender * ff, ff), ff)],
+            send_sem=y_send.at[len(y_kinds) + 1, dest], recv_sem=y_recv.at[len(y_kinds), sender],
+            device_id={"yax": dest}, device_id_type=pl.DeviceIdType.MESH)
+
+    x_wait("gate")
+    x_wait("up")
+
+    def feed(d, carry):
+        @pl.when(d < ys - 1)
+        def _():
+            nxt = lax.rem(y + ys - d - 1, ys)
+            n_copy(y, nxt).wait_recv()
+            n_pass(nxt, core).start()
+        j = lax.rem(y + ys - d, ys)
+
+        @pl.when(d > 0)
+        def _():
+            n_pass(j, 1 - core).wait_recv()
+        gu = jnp.dot(n_all[rows(j, quarter), :], gu_buf[...], preferred_element_type=F32)
+        gu = gu.astype(BF16).astype(F32)
         gate = gu[:, :ff]
-        act[:, pl.ds(j * ff, ff)] = (gate * jax.nn.sigmoid(gate) * gu[:, ff:]).astype(BF16)
-    y_wait("down")
-    part_scr[...] = jnp.dot(act[...], down_buf[...].reshape(ys * ff, xs * blk), preferred_element_type=F32)
+        act_scr[j] = (gate * jax.nn.sigmoid(gate) * gu[:, ff:]).astype(BF16)
+
+        @pl.when(d > 0)
+        def _():
+            act_copy(j, y).start()
+        return carry
+    lax.fori_loop(0, ys, feed, 0)
+    act[:, pl.ds(pl.multiple_of(y * ff, ff), ff)] = act_scr[y]
+    if e_done < EMBED_CHUNKS:
+        e_start(e_done)
+        e_done += 1
     y_wait("wo")
     x_wait("o")
-    part_scr[...] = part_scr[...] + jnp.dot(
+    part_scr[...] = jnp.dot(
         ox_buf[...], out_buf[...].reshape(ys * cols, xs * blk), preferred_element_type=F32)
-    x_start("rs")
+    y_wait("down")
+
+    def act_wait(d, carry):
+        act_copy(y, lax.rem(y + ys - d, ys)).wait_recv()
+        return carry
+    lax.fori_loop(1, ys, act_wait, 0)
+
+    def branch(c):
+        for i in range(chips):
+            r = pl.ds(pl.multiple_of((2 * i + c) * own, own), own)
+            rs_scr[c, i] = part_scr[r, :] + jnp.dot(
+                act[r, :], down_buf[...].reshape(ys * ff, xs * blk), preferred_element_type=F32)
+
+    def pre_copy():
+        return pltpu.make_async_remote_copy(
+            src_ref=rs_scr.at[1 - core], dst_ref=pre_buf, send_sem=pre_sem.at[0], recv_sem=pre_sem.at[1],
+            device_id={"xax": partner}, device_id_type=pl.DeviceIdType.MESH)
+
+    def rs_copy(dest, sender):
+        return pltpu.make_async_remote_copy(
+            src_ref=rs_scr.at[core, dest], dst_ref=rs_buf.at[sender], send_sem=f_send.at[1, dest],
+            recv_sem=pre_sem.at[2 + sender], device_id={"xax": 2 * dest + core},
+            device_id_type=pl.DeviceIdType.MESH)
+
+    chip = x // 2
+    branch(1 - core)
+    pre_copy().start()
+    branch(core)
+    pre_copy().wait_recv()
+    rs_scr[core] = rs_scr[core] + pre_buf[...]
+
+    def rs_start(i, carry):
+        rs_copy(lax.rem(chip + i, chips), chip).start()
+        return carry
+    lax.fori_loop(1, chips, rs_start, 0)
+    if e_done < EMBED_CHUNKS:
+        e_start(e_done)
+        e_done += 1
+
+    def rs_wait(i, carry):
+        rs_copy(chip, lax.rem(chip + chips - i, chips)).wait_recv()
+        return carry
+    lax.fori_loop(1, chips, rs_wait, 0)
+    rs_buf[chip] = rs_scr[core, chip]
+    res = h_buf[rows(x, own), :].astype(F32) + jnp.sum(rs_buf[...], axis=0)
+    f_buf[rows(mine, own), :] = layer_norm(res, gf_buf[...]).astype(BF16)
+
+    def f_rows(sy, sx):
+        return f_buf.at[rows(sy * xs + sx, own), :]
+
+    def f_recv_of(sy, sx):
+        return f_recv.at[sy * xs + sx]
+
+    def fx_copy(dest, sx):
+        return pltpu.make_async_remote_copy(
+            src_ref=f_rows(y, sx), dst_ref=f_rows(y, sx), send_sem=f_send.at[0, dest // 2],
+            recv_sem=f_recv_of(y, sx), device_id={"xax": dest}, device_id_type=pl.DeviceIdType.MESH)
+
+    def fy_copy(dest, sy, sx):
+        return pltpu.make_async_remote_copy(
+            src_ref=f_rows(sy, sx), dst_ref=f_rows(sy, sx), send_sem=fy_send.at[sx // 2, dest],
+            recv_sem=f_recv_of(sy, sx), device_id={"yax": dest}, device_id_type=pl.DeviceIdType.MESH)
+
+    def fp_copy(sy, sx):
+        return pltpu.make_async_remote_copy(
+            src_ref=f_rows(sy, sx), dst_ref=f_rows(sy, sx), send_sem=fp_send.at[sy, sx // 2],
+            recv_sem=f_recv_of(sy, sx), device_id={"xax": partner}, device_id_type=pl.DeviceIdType.MESH)
+
+    def fx_start(i, carry):
+        fx_copy(lax.rem(x + 2 * i, xs), x).start()
+        return carry
+    lax.fori_loop(1, chips, fx_start, 0)
+
+    def f_spread(i, carry):
+        sx = lax.rem(x + xs - 2 * i, xs)
+
+        @pl.when(i > 0)
+        def _():
+            fx_copy(x, sx).wait_recv()
+
+        def over_y(d, c2):
+            fy_copy(lax.rem(y + d, ys), y, sx).start()
+            return c2
+        lax.fori_loop(1, ys, over_y, 0)
+        fp_copy(y, sx).start()
+        return carry
+    lax.fori_loop(0, 1, f_spread, 0)
     while e_done < EMBED_CHUNKS:
         e_start(e_done)
         e_done += 1
-    x_wait("gf")
-    x_wait("rs")
-    res = h_buf[rows(x, own), :].astype(F32) + jnp.sum(rs_buf[...], axis=0)
-    mine = y * xs + x
-    f_buf[rows(mine, own), :] = layer_norm(res, gf_buf[...]).astype(BF16)
-
-    chips = xs // 2
-
-    def f_copy(dy, dx, src_y, src_x):
-        r = rows(src_y * xs + src_x, own)
-        return pltpu.make_async_remote_copy(
-            src_ref=f_buf.at[r, :], dst_ref=f_buf.at[r, :],
-            send_sem=f_send.at[dy * xs + dx], recv_sem=f_recv.at[src_y * xs + src_x],
-            device_id={"yax": dy, "xax": dx}, device_id_type=pl.DeviceIdType.MESH)
-
-    def p_copy(src_y, src_x):
-        r = rows(src_y * xs + src_x, own)
-        return pltpu.make_async_remote_copy(
-            src_ref=f_buf.at[r, :], dst_ref=f_buf.at[r, :],
-            send_sem=p_send.at[src_y * xs + src_x], recv_sem=p_recv.at[src_y * xs + src_x],
-            device_id={"xax": partner}, device_id_type=pl.DeviceIdType.MESH)
-
-    def plane_peer(i, sign):
-        py = lax.rem(y + ys + sign * (i // chips), ys)
-        px = lax.rem(x + xs + sign * 2 * lax.rem(i, chips), xs)
-        return py, px
-
-    def f_start(i, carry):
-        py, px = plane_peer(i, 1)
-        f_copy(py, px, y, x).start()
-        return carry
-    lax.fori_loop(1, ys * chips, f_start, 0)
-    p_copy(y, x).start()
+    lax.fori_loop(1, chips, f_spread, 0)
 
     e_own().wait()
     for c in range(EMBED_CHUNKS):
@@ -386,16 +548,16 @@
 
         def forward(i, c2):
             sx = lax.rem(x + xs - 2 * i, xs)
-
-            @pl.when(jnp.logical_or(dy > 0, i > 0))
-            def _():
-                f_copy(y, x, j, sx).wait_recv()
-                p_copy(j, sx).start()
+            fy_copy(y, j, sx).wait_recv()
+            fp_copy(j, sx).start()
             return c2
-        lax.fori_loop(0, chips, forward, 0)
+
+        @pl.when(dy > 0)
+        def _():
+            lax.fori_loop(0, chips, forward, 0)
 
         def arrive(i, c2):
-            p_copy(j, lax.rem(partner + xs - 2 * i, xs)).wait_recv()
+            fp_copy(j, lax.rem(partner + xs - 2 * i, xs)).wait_recv()
             return c2
         lax.fori_loop(0, chips, arrive, 0)
         slot = lax.rem(dy, 2)
@@ -413,22 +575,43 @@
         return carry
     lax.fori_loop(0, ys, head, 0)
 
-    def s_copy(dest_y, dest_x, src):
-        return pltpu.make_async_remote_copy(
-            src_ref=st_scr, dst_ref=st_buf.at[src], send_sem=s_send.at[dest_y * xs + dest_x],
-            recv_sem=s_recv.at[src], device_id={"yax": dest_y, "xax": dest_x},
-            device_id_type=pl.DeviceIdType.MESH)
-
-    def s_start(i, carry):
-        s_copy(lax.rem(y + i // xs, ys), lax.rem(x + lax.rem(i, xs), xs), mine).start()
-        return carry
-    lax.fori_loop(1, ys * xs, s_start, 0)
-    st_buf[mine] = st_scr[...]
+    def sx_copy(dest, src):
+        return pltpu.make_async_remote_copy(
+            src_ref=st_scr, dst_ref=sx_buf.at[src], send_sem=sx_send.at[dest], recv_sem=sx_recv.at[src],
+            device_id={"xax": dest}, device_id_type=pl.DeviceIdType.MESH)
+
+    def sy_copy(dest, src):
+        return pltpu.make_async_remote_copy(
+            src_ref=sy_scr, dst_ref=sy_buf.at[src], send_sem=sy_send.at[dest], recv_sem=sy_recv.at[src],
+            device_id={"yax": dest}, device_id_type=pl.DeviceIdType.MESH)
+
+    def combine(buf):
+        tops = buf[:, 0, :]
+        best = jnp.max(tops, axis=0, keepdims=True)
+        return best, jnp.sum(buf[:, 1, :] * jnp.exp(tops - best), axis=0, keepdims=True)
+
+    def sx_start(d, carry):
+        sx_copy(lax.rem(x + d, xs), x).start()
+        return carry
+    lax.fori_loop(1, xs, sx_start, 0)
+    sx_buf[x] = st_scr[...]
 
     for name in x_kinds:
-        x_drain(name)
+        if name in gathers:
+            g_drain(name)
+        else:
+            x_drain(name)
     for name in y_kinds:
         y_drain(name)
+
+    def yn_drain(d, carry):
+        dest = lax.rem(y + d, ys)
+        n_copy(dest, y).wait_send()
+        n_pass(dest, core).wait_send()
+        act_copy(dest, y).wait_send()
+        return carry
+    lax.fori_loop(1, ys, yn_drain, 0)
+    pre_copy().wait_send()
     for c in range(EMBED_CHUNKS):
         def e_drain(d, carry, c=c):
             e_copy(c, lax.rem(x + d, xs), x).wait_send()
@@ -436,32 +619,50 @@
         lax.fori_loop(1, xs, e_drain, 0)
 
     def f_drain(i, carry):
-        py, px = plane_peer(i, 1)
-        f_copy(py, px, y, x).wait_send()
-        return carry
-    lax.fori_loop(1, ys * chips, f_drain, 0)
-
-    def p_drain(i, carry):
-        py, px = plane_peer(i, 1)
-        p_copy(py, px).wait_send()
-        return carry
-    lax.fori_loop(0, ys * chips, p_drain, 0)
-
-    def s_wait(i, carry):
-        sy = lax.rem(y + ys - i // xs, ys)
-        sx = lax.rem(x + xs - lax.rem(i, xs), xs)
-        s_copy(y, x, sy * xs + sx).wait_recv()
-        return carry
-    lax.fori_loop(1, ys * xs, s_wait, 0)
-    tops = st_buf[:, 0, :]
-    best = jnp.max(tops, axis=0, keepdims=True)
-    whole = jnp.sum(st_buf[:, 1, :] * jnp.exp(tops - best), axis=0, keepdims=True)
+        @pl.when(i > 0)
+        def _():
+            rs_copy(lax.rem(chip + i, chips), chip).wait_send()
+            fx_copy(lax.rem(x + 2 * i, xs), x).wait_send()
+        sx = lax.rem(x + xs - 2 * i, xs)
+
+        def over_y(d, c2):
+            other = lax.rem(y + d, ys)
+
+            @pl.when(d > 0)
+            def _():
+                fy_copy(other, y, sx).wait_send()
+            fp_copy(other, sx).wait_send()
+            return c2
+        lax.fori_loop(0, ys, over_y, 0)
+        return carry
+    lax.fori_loop(0, chips, f_drain, 0)
+
+    def sx_wait(d, carry):
+        sx_copy(x, lax.rem(x + xs - d, xs)).wait_recv()
+        return carry
+    lax.fori_loop(1, xs, sx_wait, 0)
+    best, whole = combine(sx_buf)
+    sy_scr[0:1, :] = best
+    sy_scr[1:2, :] = whole
+
+    def sy_start(d, carry):
+        sy_copy(lax.rem(y + d, ys), y).start()
+        return carry
+    lax.fori_loop(1, ys, sy_start, 0)
+    sy_buf[y] = sy_scr[...]
+
+    def sx_drain(d, carry):
+        sx_copy(lax.rem(x + d, xs), x).wait_send()
+        return carry
+    lax.fori_loop(1, xs, sx_drain, 0)
+
+    def sy_wait(d, carry):
+        sy_copy(y, lax.rem(y + ys - d, ys)).wait_recv()
+        sy_copy(lax.rem(y + d, ys), y).wait_send()
+        return carry
+    lax.fori_loop(1, ys, sy_wait, 0)
+    best, whole = combine(sy_buf)
     norm_out[...] = best + jnp.log(whole)
-
-    def s_drain(i, carry):
-        s_copy(lax.rem(y + i // xs, ys), lax.rem(x + lax.rem(i, xs), xs), mine).wait_send()
-        return carry
-    lax.fori_loop(1, ys * xs, s_drain, 0)
     for dy in range(max(ys - 2, 0), ys):
         z_copy(lax.rem(y + ys - dy, ys), dy % 2).wait()
 
@@ -492,8 +693,8 @@
         vmem = pl.BlockSpec(memory_space=pltpu.VMEM)
         smem = pl.BlockSpec(memory_space=pltpu.SMEM)
         dma = pltpu.SemaphoreType.DMA
-        nx = 13
-        all_n = ys * xs
+        nx = 12
+        chips = xs // 2
         scratch = [
             pltpu.VMEM((groups, per, head_dim, slots), BF16),
             pltpu.VMEM((groups, per, head_dim, slots), BF16),
@@ -502,11 +703,11 @@
             pltpu.VMEM((1, width), F32),
             pltpu.VMEM((w_query.shape[1], blk), BF16),
             pltpu.VMEM((ys, cols, width), BF16),
-            pltpu.VMEM((ys, width, 2 * ff), BF16),
+            pltpu.VMEM((width, 2 * ff), BF16),
             pltpu.VMEM((ys, ff, width), BF16),
             pltpu.VMEM((ys, cols, width), BF16),
             pltpu.VMEM((2 * head_dim, width), BF16),
-            pltpu.VMEM((quarter, width), BF16),
+            pltpu.VMEM((batch, width), BF16),
             pltpu.VMEM((quarter, ys * cols), BF16),
             pltpu.VMEM((xs, own, ys * cols), BF16),
             pltpu.VMEM((own * heads, head_dim), F32),
@@ -517,19 +718,25 @@
             pltpu.VMEM((own * heads, head_dim), F32),
             pltpu.VMEM((xs, own, ys * cols), BF16),
             pltpu.VMEM((quarter, ys * cols), BF16),
+            pltpu.VMEM((ys, quarter, ff), BF16),
             pltpu.VMEM((quarter, ys * ff), BF16),
             pltpu.VMEM((quarter, width), F32),
-            pltpu.VMEM((xs, own, width), F32),
+            pltpu.VMEM((chips, own, width), F32),
+            pltpu.VMEM((2, chips, own, width), F32),
+            pltpu.VMEM((chips, own, width), F32),
             pltpu.VMEM((batch, width), BF16),
             pltpu.VMEM((window, width), BF16),
             pltpu.VMEM((vocab, width), BF16),
             pltpu.VMEM((2, vocab, quarter), F32),
             pltpu.VMEM((2, batch), F32),
-            pltpu.VMEM((all_n, 2, batch), F32),
+            pltpu.VMEM((xs, 2, batch), F32),
+            pltpu.VMEM((2, batch), F32),
+            pltpu.VMEM((ys, 2, batch), F32),
             dma((2, groups)), dma((nx + 1,)), dma((2,)),
-            dma((nx, xs)), dma((nx, xs)), dma((4, ys)), dma((4, ys)),
+            dma((nx, xs)), dma((nx, xs)), dma((5, xs)), dma((5, ys)), dma((4, ys)),
             dma((EMBED_CHUNKS, xs)), dma((EMBED_CHUNKS, xs)),
-            dma((all_n,)), dma((all_n,)), dma((all_n,)), dma((all_n,)), dma((all_n,)), dma((all_n,)),
+            dma((ys, 2)), dma((ys,)), dma((2 + chips,)), dma((2, chips)), dma((ys * xs,)),
+            dma((chips, ys)), dma((ys, chips)), dma((xs,)), dma((xs,)), dma((ys,)), dma((ys,)),
         ]
         cfg = (ys, xs, own, vocab, shift)
         key_new, value_new, logits, norm = pl.pallas_call(

time: 127 us -> 104 us (0.82)
  Pallas kernels: 118 us -> 95.3 us
    pallas_call x1, Pallas kernels: 118 us -> 95.3 us  [local_step(): pl.pallas_call(functools.partial(kernel, cfg), name='decode_layer', out_s...]
where the time goes in v3:
time: 104 us
  Pallas kernels  95.3 us (92%)
  other arithmetic  6.44 us (6%)
  local copies, waits for them, and re-layouts  1.8 us (2%)
    pallas_call x1, Pallas kernels, local_step(): pl.pallas_call(functools.partial(kernel, cfg), name='decode_layer', out_s...  95.3 us
    transpose x1, other arithmetic, local_step(): return (key_new, value_new, (logits - norm).T, log_norm)  6.44 us

profile of v3, /device:TPU:97, one launch (start us, length us, event | category | flops | bytes accessed | tf_op | source)
XLA Modules:
  0.0 104.2 jit_solution(7104887926917625679)
XLA Ops:
  0.6 95.3 %decode_layer.1 = (bf16[32,64]{1,0:T(8,128)(2,1)}, bf16[32,64]{1,0:T(8,128)(2,1)}, f32[1572,1024]{1,0:T(8,128)}, f32[1,1024]{1,0:T(1,128)}) custom-call(s32[1024]{0:T(1024)} %lens.1, bf16[1024,128]{1,0:T(8,128)(2,1)} %hidden.1, bf16[32,64,4096]{2,1,0:T(8,128)(2,1)} %bitcast.9, bf16[32,64,4096]{2,1,0:T(8,128)(2,1)} %bitcast.10, f32[1,128]{1,0:T(1,128)} %bitcast.15, ...), custom_call_target="tpu_custom_call" | custom-call | tf_op jit(solution)/shard_map/decode_layer/pallas_call | solution.py:742
  95.9 0.0 copy-start.2
  95.9 0.0 copy-start.1
  95.9 0.0 copy-start
  95.9 6.4 %subtract_bitcast_fusion = f32[1024,1572]{0,1:T(8,128)} fusion(f32[1572,1024]{1,0:T(8,128)} %get-tuple-element.10, f32[1024]{0:T(1024)} %bitcast.13), kind=kLoop, calls=%fused_computation | loop fusion | flops 1609728 | bytes 12881920 | tf_op jit(solution)/shard_map/transpose | solution.py:759
  102.4 0.0 copy-done.2
  102.4 0.6 copy.22
  103.0 0.0 copy-done.1
  103.0 0.6 copy.23
  103.6 0.0 copy-done
  103.6 0.6 copy.24
Async XLA Ops:
  95.9 6.5 %copy-start.2 = (bf16[32,64]{1,0:T(8,128)(2,1)S(1)}, bf16[32,64]{1,0:T(8,128)(2,1)}, u32[]{:S(2)}) copy-start(bf16[32,64]{1,0:T(8,128)(2,1)} %get-tuple-element.16) | copy-start | bytes 12292
  95.9 7.1 %copy-start.1 = (bf16[32,64]{1,0:T(8,128)(2,1)S(1)}, bf16[32,64]{1,0:T(8,128)(2,1)}, u32[]{:S(2)}) copy-start(bf16[32,64]{1,0:T(8,128)(2,1)} %get-tuple-element.17) | copy-start | bytes 12292
  95.9 7.7 %copy-start = (f32[1,1024]{1,0:T(1,128)S(1)}, f32[1,1024]{1,0:T(1,128)}, u32[]{:S(2)}) copy-start(f32[1,1024]{1,0:T(1,128)} %get-tuple-element.11) | copy-start | bytes 12292

commit v4 on v3

--- a/solution.py
+++ b/solution.py
@@ -13,7 +13,8 @@
 F32 = jnp.float32
 BF16 = jnp.bfloat16
 NT = (((1,), (1,)), ((), ()))
-EMBED_CHUNKS = 8
+EMBED_CHUNKS = 16
+EMBED_GROUPS = 4
 
 
 def layer_norm(values_in, gain):
@@ -24,8 +25,7 @@
 
 
 def row_chunks(total, count):
-    tiles = total // 8
-    cuts = [8 * (tiles * i // count) for i in range(count + 1)]
+    cuts = [16 * (total // 16 * i // count) for i in range(count)] + [total]
     return [(cuts[i], cuts[i + 1] - cuts[i]) for i in range(count)]
 
 
@@ -34,7 +34,7 @@
            k_out, v_out, logits_out, norm_out,
            k_buf, v_buf, h_buf, ga_buf, gf_buf, wqt, wq_buf, gu_buf, down_buf, out_buf, kv_buf,
            n_all, q_scr, qx_buf, q2d, snew, krep, vrep, s_scr, od_scr, o_scr, ox_buf, act_scr, act, part_scr,
-           pre_buf, rs_scr, rs_buf, f_buf, e_buf, e_al, z_scr, st_scr, sx_buf, sy_scr, sy_buf,
+           pre_buf, rs_scr, rs_buf, f_buf, e_buf, z_scr, st_scr, k_scr, v_scr, norm_scr, sx_buf, sy_scr, sy_buf,
            kv_sem, own_sem, z_sem, x_send, x_recv, g_send, y_send, y_recv, e_send, e_recv,
            n_recv, n_fwd, pre_sem, f_send, f_recv, fy_send, fp_send, sx_send, sx_recv, sy_send, sy_recv):
     ys, xs, own, vocab, shift = cfg
@@ -238,6 +238,7 @@
         x_start(name)
     for name in ("wk", "wv", "gf"):
         g_start(name)
+    e_start(0)
     e_own().start()
 
     def start_cache_v(g, carry):
@@ -288,7 +289,8 @@
     y_start("wo")
     x_wait("down")
     y_start("down")
-    e_start(0)
+    for c in range(1, 6):
+        e_start(c)
 
     row_id = lax.broadcasted_iota(jnp.int32, (own, 4 * half), 0)
     first_row = (y * xs + x) * own
@@ -311,8 +313,12 @@
     s1 = sin_a[:, :half]
     key = jnp.concatenate([k1 * c1 - k2 * s1, k2 * c1 + k1 * s1], axis=1).astype(BF16)
     value = kv[:, head_dim:].astype(BF16)
-    k_out[...] = key
-    v_out[...] = value
+    k_scr[...] = key
+    v_scr[...] = value
+    small_outs = [pltpu.make_async_copy(k_scr, k_out, z_sem.at[EMBED_GROUPS]),
+                  pltpu.make_async_copy(v_scr, v_out, z_sem.at[EMBED_GROUPS + 1])]
+    for copy in small_outs:
+        copy.start()
     for h in range(heads):
         krep[pl.ds(h, own, stride=heads), :] = key.astype(F32)
         vrep[pl.ds(h, own, stride=heads), :] = value.astype(F32)
@@ -376,18 +382,13 @@
                 + add[s * heads:(s + 1) * heads, :])
         return carry
 
-    e_done = 1
-    steps = 4
-    for i in range(steps):
-        lax.fori_loop(i * groups // steps, (i + 1) * groups // steps, attend, 0)
-        if e_done < EMBED_CHUNKS:
-            e_start(e_done)
-            e_done += 1
+    lax.fori_loop(0, groups, attend, 0)
     for xc in range(xs // 2):
         parts = [od_scr[pl.ds(xc * ys + yc, own, stride=heads), :] for yc in range(ys)]
         o_scr[2 * xc] = jnp.concatenate([p[:, :half] for p in parts], axis=1).astype(BF16)
         o_scr[2 * xc + 1] = jnp.concatenate([p[:, half:] for p in parts], axis=1).astype(BF16)
     x_start("o")
+    e_start(6)
 
     def act_copy(dest, sender):
         return pltpu.make_async_remote_copy(
@@ -420,9 +421,7 @@
         return carry
     lax.fori_loop(0, ys, feed, 0)
     act[:, pl.ds(pl.multiple_of(y * ff, ff), ff)] = act_scr[y]
-    if e_done < EMBED_CHUNKS:
-        e_start(e_done)
-        e_done += 1
+    e_start(7)
     y_wait("wo")
     x_wait("o")
     part_scr[...] = jnp.dot(
@@ -434,11 +433,12 @@
         return carry
     lax.fori_loop(1, ys, act_wait, 0)
 
+    down_all = down_buf[...].reshape(ys * ff, xs * blk)
+    part_scr[...] = part_scr[...] + jnp.dot(act[...], down_all, preferred_element_type=F32)
+
     def branch(c):
         for i in range(chips):
-            r = pl.ds(pl.multiple_of((2 * i + c) * own, own), own)
-            rs_scr[c, i] = part_scr[r, :] + jnp.dot(
-                act[r, :], down_buf[...].reshape(ys * ff, xs * blk), preferred_element_type=F32)
+            rs_scr[c, i] = part_scr[pl.ds(pl.multiple_of((2 * i + c) * own, own), own), :]
 
     def pre_copy():
         return pltpu.make_async_remote_copy(
@@ -462,9 +462,7 @@
         rs_copy(lax.rem(chip + i, chips), chip).start()
         return carry
     lax.fori_loop(1, chips, rs_start, 0)
-    if e_done < EMBED_CHUNKS:
-        e_start(e_done)
-        e_done += 1
+    e_start(8)
 
     def rs_wait(i, carry):
         rs_copy(chip, lax.rem(chip + chips - i, chips)).wait_recv()
@@ -514,87 +512,9 @@
         fp_copy(y, sx).start()
         return carry
     lax.fori_loop(0, 1, f_spread, 0)
-    while e_done < EMBED_CHUNKS:
-        e_start(e_done)
-        e_done += 1
+    for c in range(9, EMBED_CHUNKS):
+        e_start(c)
     lax.fori_loop(1, chips, f_spread, 0)
-
-    e_own().wait()
-    for c in range(EMBED_CHUNKS):
-        def e_wait(d, carry, c=c):
-            e_copy(c, x, lax.rem(x + xs - d, xs)).wait_recv()
-            return carry
-        lax.fori_loop(1, xs, e_wait, 0)
-    if shift:
-        @pl.when(core == 1)
-        def _():
-            for r0 in range(0, vocab, 256):
-                n = min(256, vocab - r0)
-                e_al[pl.ds(r0, n), :] = e_buf[pl.ds(r0 + shift, n), :]
-
-        @pl.when(core == 0)
-        def _():
-            for r0 in range(0, vocab, 256):
-                n = min(256, vocab - r0)
-                e_al[pl.ds(r0, n), :] = e_buf[pl.ds(r0, n), :]
-    else:
-        e_al[...] = e_buf[...]
-
-    def z_copy(j, slot):
-        return pltpu.make_async_copy(z_scr.at[slot], logits_out.at[:, rows(j, quarter)], z_sem.at[slot])
-
-    def head(dy, carry):
-        j = lax.rem(y + ys - dy, ys)
-
-        def forward(i, c2):
-            sx = lax.rem(x + xs - 2 * i, xs)
-            fy_copy(y, j, sx).wait_recv()
-            fp_copy(j, sx).start()
-            return c2
-
-        @pl.when(dy > 0)
-        def _():
-            lax.fori_loop(0, chips, forward, 0)
-
-        def arrive(i, c2):
-            fp_copy(j, lax.rem(partner + xs - 2 * i, xs)).wait_recv()
-            return c2
-        lax.fori_loop(0, chips, arrive, 0)
-        slot = lax.rem(dy, 2)
-
-        @pl.when(dy >= 2)
-        def _():
-            z_copy(j, slot).wait()
-        z = lax.dot_general(e_al[...], f_buf[rows(j, quarter), :], NT, preferred_element_type=F32)
-        z_scr[slot] = z
-        z_copy(j, slot).start()
-        top = jnp.max(z, axis=0, keepdims=True)
-        tot = jnp.sum(jnp.exp(z - top), axis=0, keepdims=True)
-        st_scr[0:1, rows(j, quarter)] = top
-        st_scr[1:2, rows(j, quarter)] = tot
-        return carry
-    lax.fori_loop(0, ys, head, 0)
-
-    def sx_copy(dest, src):
-        return pltpu.make_async_remote_copy(
-            src_ref=st_scr, dst_ref=sx_buf.at[src], send_sem=sx_send.at[dest], recv_sem=sx_recv.at[src],
-            device_id={"xax": dest}, device_id_type=pl.DeviceIdType.MESH)
-
-    def sy_copy(dest, src):
-        return pltpu.make_async_remote_copy(
-            src_ref=sy_scr, dst_ref=sy_buf.at[src], send_sem=sy_send.at[dest], recv_sem=sy_recv.at[src],
-            device_id={"yax": dest}, device_id_type=pl.DeviceIdType.MESH)
-
-    def combine(buf):
-        tops = buf[:, 0, :]
-        best = jnp.max(tops, axis=0, keepdims=True)
-        return best, jnp.sum(buf[:, 1, :] * jnp.exp(tops - best), axis=0, keepdims=True)
-
-    def sx_start(d, carry):
-        sx_copy(lax.rem(x + d, xs), x).start()
-        return carry
-    lax.fori_loop(1, xs, sx_start, 0)
-    sx_buf[x] = st_scr[...]
 
     for name in x_kinds:
         if name in gathers:
@@ -612,6 +532,87 @@
         return carry
     lax.fori_loop(1, ys, yn_drain, 0)
     pre_copy().wait_send()
+    for copy in small_outs:
+        copy.wait()
+
+    def f_from_y(d, carry):
+        sy = lax.rem(y + ys - d, ys)
+
+        def one(i, c2):
+            sx = lax.rem(x + xs - 2 * i, xs)
+            fy_copy(y, sy, sx).wait_recv()
+            fp_copy(sy, sx).start()
+            return c2
+        lax.fori_loop(0, chips, one, 0)
+        return carry
+    lax.fori_loop(1, ys, f_from_y, 0)
+
+    def f_from_core(d, carry):
+        sy = lax.rem(y + ys - d, ys)
+
+        def one(i, c2):
+            fp_copy(sy, lax.rem(partner + xs - 2 * i, xs)).wait_recv()
+            return c2
+        lax.fori_loop(0, chips, one, 0)
+        return carry
+    lax.fori_loop(0, ys, f_from_core, 0)
+
+    each = EMBED_CHUNKS // EMBED_GROUPS
+
+    def group_rows(g):
+        r0 = e_parts[g * each][0]
+        last = e_parts[(g + 1) * each - 1]
+        return r0, last[0] + last[1] - r0
+
+    def z_copy(g):
+        r0, n = group_rows(g)
+        return pltpu.make_async_copy(z_scr.at[pl.ds(r0, n), :], logits_out.at[pl.ds(r0, n), :], z_sem.at[g])
+
+    skip = core * shift
+    top = jnp.full((1, f_buf.shape[0]), -jnp.inf, F32)
+    total = jnp.zeros((1, f_buf.shape[0]), F32)
+    e_own().wait()
+    for g in range(EMBED_GROUPS):
+        for c in range(g * each, (g + 1) * each):
+            def e_wait(d, carry, c=c):
+                e_copy(c, x, lax.rem(x + xs - d, xs)).wait_recv()
+                return carry
+            lax.fori_loop(1, xs, e_wait, 0)
+        r0, n = group_rows(g)
+        z = lax.dot_general(e_buf[pl.ds(r0, n), :], f_buf[...], NT, preferred_element_type=F32)
+        z_scr[pl.ds(r0, n), :] = z
+        z_copy(g).start()
+        z = z_scr[pl.ds(r0, n), :]
+        if shift and g in (0, EMBED_GROUPS - 1):
+            index = lax.broadcasted_iota(jnp.int32, (n, 1), 0) + r0
+            z = jnp.where(jnp.logical_and(index >= skip, index < skip + vocab), z, -jnp.inf)
+        top_g = jnp.maximum(top, jnp.max(z, axis=0, keepdims=True))
+        total = total * jnp.exp(top - top_g) + jnp.sum(jnp.exp(z - top_g), axis=0, keepdims=True)
+        top = top_g
+    st_scr[0:1, :] = top
+    st_scr[1:2, :] = total
+
+    def sx_copy(dest, src):
+        return pltpu.make_async_remote_copy(
+            src_ref=st_scr, dst_ref=sx_buf.at[src], send_sem=sx_send.at[dest], recv_sem=sx_recv.at[src],
+            device_id={"xax": dest}, device_id_type=pl.DeviceIdType.MESH)
+
+    def sy_copy(dest, src):
+        return pltpu.make_async_remote_copy(
+            src_ref=sy_scr, dst_ref=sy_buf.at[src], send_sem=sy_send.at[dest], recv_sem=sy_recv.at[src],
+            device_id={"yax": dest}, device_id_type=pl.DeviceIdType.MESH)
+
+    def combine(buf):
+        tops = buf[:, 0, :]
+        best = jnp.max(tops, axis=0, keepdims=True)
+        return best, jnp.sum(buf[:, 1, :] * jnp.exp(tops - best), axis=0, keepdims=True)
+
+    def sx_start(d, carry):
+        sx_copy(lax.rem(x + d, xs), x).start()
+        return carry
+    lax.fori_loop(1, xs, sx_start, 0)
+    sx_buf[x] = st_scr[...]
+
     for c in range(EMBED_CHUNKS):
         def e_drain(d, carry, c=c):
             e_copy(c, lax.rem(x + d, xs), x).wait_send()
@@ -662,9 +663,32 @@
         return carry
     lax.fori_loop(1, ys, sy_wait, 0)
     best, whole = combine(sy_buf)
-    norm_out[...] = best + jnp.log(whole)
-    for dy in range(max(ys - 2, 0), ys):
-        z_copy(lax.rem(y + ys - dy, ys), dy % 2).wait()
+    norm_scr[...] = best + jnp.log(whole)
+    norm_copy = pltpu.make_async_copy(norm_scr, norm_out, z_sem.at[EMBED_GROUPS + 2])
+    norm_copy.start()
+    for g in range(EMBED_GROUPS):
+        z_copy(g).wait()
+    norm_copy.wait()
+
+
+def finish_kernel(shift, z_ref, next_ref, norm, key, value, out_ref, k_out, v_out, norm_out):
+    n = z_ref.shape[0]
+    if shift:
+        odd = lax.rem(lax.axis_index("xax"), 2) == 1
+
+        @pl.when(odd)
+        def _():
+            out_ref[pl.ds(0, n - shift), :] = z_ref[pl.ds(shift, n - shift), :] - norm[...]
+            out_ref[pl.ds(n - shift, shift), :] = next_ref[pl.ds(0, shift), :] - norm[...]
+
+        @pl.when(jnp.logical_not(odd))
+        def _():
+            out_ref[...] = z_ref[...] - norm[...]
+    else:
+        out_ref[...] = z_ref[...] - norm[...]
+    k_out[...] = key[...]
+    v_out[...] = value[...]
+    norm_out[...] = norm[...]
 
 
 def solution(mesh):
@@ -726,13 +750,15 @@
             pltpu.VMEM((chips, own, width), F32),
             pltpu.VMEM((batch, width), BF16),
             pltpu.VMEM((window, width), BF16),
-            pltpu.VMEM((vocab, width), BF16),
-            pltpu.VMEM((2, vocab, quarter), F32),
+            pltpu.VMEM((window, batch), F32),
             pltpu.VMEM((2, batch), F32),
+            pltpu.VMEM((own, head_dim), BF16),
+            pltpu.VMEM((own, head_dim), BF16),
+            pltpu.VMEM((1, batch), F32),
             pltpu.VMEM((xs, 2, batch), F32),
             pltpu.VMEM((2, batch), F32),
             pltpu.VMEM((ys, 2, batch), F32),
-            dma((2, groups)), dma((nx + 1,)), dma((2,)),
+            dma((2, groups)), dma((nx + 1,)), dma((EMBED_GROUPS + 3,)),
             dma((nx, xs)), dma((nx, xs)), dma((5, xs)), dma((5, ys)), dma((4, ys)),
             dma((EMBED_CHUNKS, xs)), dma((EMBED_CHUNKS, xs)),
             dma((ys, 2)), dma((ys,)), dma((2 + chips,)), dma((2, chips)), dma((ys * xs,)),
@@ -745,18 +771,39 @@
             out_shape=(
                 jax.ShapeDtypeStruct((own, head_dim), BF16),
                 jax.ShapeDtypeStruct((own, head_dim), BF16),
-                jax.ShapeDtypeStruct((vocab, batch), F32),
+                jax.ShapeDtypeStruct((window, batch), F32),
                 jax.ShapeDtypeStruct((1, batch), F32)),
             in_specs=[smem, any_spec, any_spec, any_spec, any_spec, any_spec, vmem] + [any_spec] * 7 + [vmem],
-            out_specs=(vmem, vmem, any_spec, vmem),
+            out_specs=(any_spec, any_spec, any_spec, any_spec),
             scratch_shapes=scratch,
             compiler_params=pltpu.CompilerParams(
                 collective_id=0, has_side_effects=True, vmem_limit_bytes=67043328),
         )(cache_len, hidden, k_cache.transpose(0, 2, 1), v_cache.transpose(0, 2, 1),
           g_attn[None, :], g_final[None, :], w_query, w_key.T, w_value.T, w_gate, w_up, w_out, w_down,
           embedding, freq)
-        log_norm = norm[0]
-        return key_new, value_new, (logits - norm).T, log_norm
+        step = min(320, window)
+        steps = -(-window // step)
+
+        def fixed(shape):
+            return pl.BlockSpec(shape, lambda i: (0, 0))
+        log_probs, key_new, value_new, norm = pl.pallas_call(
+            functools.partial(finish_kernel, shift),
+            name="finish",
+            grid=(steps,),
+            out_shape=(
+                jax.ShapeDtypeStruct((vocab, batch), F32),
+                jax.ShapeDtypeStruct((own, head_dim), BF16),
+                jax.ShapeDtypeStruct((own, head_dim), BF16),
+                jax.ShapeDtypeStruct((1, batch), F32)),
+            in_specs=[
+                pl.BlockSpec((step, batch), lambda i: (i, 0)),
+                pl.BlockSpec((8, batch), lambda i: (jnp.minimum((i + 1) * (step // 8), window // 8 - 1), 0)),
+                fixed((1, batch)), fixed((own, head_dim)), fixed((own, head_dim))],
+            out_specs=(
+                pl.BlockSpec((step, batch), lambda i: (i, 0)),
+                fixed((own, head_dim)), fixed((own, head_dim)), fixed((1, batch))),
+        )(logits, logits, norm, key_new, value_new)
+        return key_new, value_new, log_probs.T, norm[0]
 
     in_specs = (P("dp", "xax"), P("dp"), row_spec, row_spec, P("xax"), P("xax", "yax"),
                 P("xax", None), P("xax", None), P("xax", "yax"), P("xax", "yax"),

time: 104 us -> 104 us (level)
  Pallas kernels: 95.3 us -> 104 us
  other arithmetic: 6.44 us -> 0 us
  local copies, waits for them, and re-layouts: 1.8 us -> 0 us
    pallas_call x0 -> x1, Pallas kernels: none -> 7.45 us  [local_step(): pl.pallas_call(functools.partial(finish_kernel, shift), name='finish', gr...]
    transpose x1 -> x0, other arithmetic: 6.44 us -> none  [local_step(): return (key_new, value_new, (logits - norm).T, log_norm)]
    unnamed x9 -> x0, local copies, waits for them, and re-layouts: 1.8 us -> none
where the time goes in v4:
time: 104 us
  Pallas kernels  104 us (100%)
    pallas_call x1, Pallas kernels, local_step(): pl.pallas_call(functools.partial(kernel, cfg), name='decode_layer', out_s...  96.1 us
    pallas_call x1, Pallas kernels, local_step(): pl.pallas_call(functools.partial(finish_kernel, shift), name='finish', gr...  7.45 us

profile of v4, /device:TPU:97, one launch (start us, length us, event | category | flops | bytes accessed | tf_op | source)
XLA Modules:
  0.0 104.2 jit_solution(1500970996826552722)
XLA Ops:
  0.6 96.1 %decode_layer.1 = (bf16[32,64]{1,0:T(8,128)(2,1)}, bf16[32,64]{1,0:T(8,128)(2,1)}, f32[1576,1024]{1,0:T(8,128)}, f32[1,1024]{1,0:T(1,128)}) custom-call(s32[1024]{0:T(1024)} %lens.1, bf16[1024,128]{1,0:T(8,128)(2,1)} %hidden.1, bf16[32,64,4096]{2,1,0:T(8,128)(2,1)} %bitcast.8, bf16[32,64,4096]{2,1,0:T(8,128)(2,1)} %bitcast.9, f32[1,128]{1,0:T(1,128)} %bitcast.12, ...), custom_call_target="tpu_custom_call" | custom-call | tf_op jit(solution)/shard_map/decode_layer/pallas_call | solution.py:768
  96.8 7.5 %finish.1 = (f32[1572,1024]{1,0:T(8,128)}, bf16[32,64]{1,0:T(8,128)(2,1)}, bf16[32,64]{1,0:T(8,128)(2,1)}, f32[1,1024]{1,0:T(1,128)}) custom-call(f32[1576,1024]{1,0:T(8,128)} %get-tuple-element.12.z_ref.next_ref, f32[1576,1024]{1,0:T(8,128)} %get-tuple-element.12.z_ref.next_ref, f32[1,1024]{1,0:T(1,128)} %get-tuple-element.13.norm, ...), custom_call_target="tpu_custom_call" | custom-call | tf_op jit(solution)/shard_map/finish/pallas_call | solution.py:789
